TPU v7x, 32 devices: a whole 2x2x4 slice. The times are simulated.
32 devices in a mesh: tok: 16 (over z, y, x), head: 2 (over core).
Axes of the slice: x: 2, y: 2, z: 4, core: 2. Of those that a mesh axis runs over, the one named last changes fastest.
Arguments:
- text_queries: bfloat16 [256, 8192], P('tok', 'head'), may hold values from -6 to 6
- text_grads: bfloat16 [256, 8192], P('tok', 'head'), may hold values from -6 to 6
- vision_keys: bfloat16 [8192, 1024], P('tok', 'head'), may hold values from -6 to 6
- video_value_rows: bfloat16 [8192, 1024], P('tok', 'head'), may hold values from -6 to 6
- vision: bfloat16 [8192, 4096], P('tok'), may hold values from -6 to 6
- lengths: int32 [8], replicated, may hold values from 16 to 48, as said below
- frame_range: int32 [8, 2], replicated, may hold values from 0 to 64, as said below
Outputs:
- query_grad: bfloat16 [256, 8192], P(None, 'head')
- key_weight_grad: float32 [4096, 1024], P('tok', 'head')
- value_weight_grad: float32 [4096, 1024], P('tok', 'head')
Inputs may be any that keep to these rules, and one draw needn't show every extreme that they name: Each segment holds at least one row; the lengths sum to 256. `frame_range`: each segment's range covers 64 // 4 frames or more, first entry below the second.
All inputs are finite; a program needn't handle non-finite values.
Results may differ from a plain program's by a relative error of at most 0.0073.
Values may be sent and summed in bfloat16 or wider, within the bound.
A program may use at most 128 MiB of HBM per device.

v0:
```python
import functools

import jax
import jax.numpy as jnp
from jax import lax
from jax.experimental import pallas as pl
from jax.experimental.pallas import tpu as pltpu
from jax.sharding import PartitionSpec as P

HEAD_WIDTH = 128
FRAME_DEV = 4
NEG_FILL = -1e30
NT = (((1,), (1,)), ((), ()))
TN = (((0,), (0,)), ((), ()))
F32 = jnp.float32
BF16 = jnp.bfloat16


def dot(a, b, dims=(((1,), (0,)), ((), ()))):
    return lax.dot_general(a, b, dims, preferred_element_type=F32)


def kernel(cfg, q_in, g_in, k_in, v_in, x_in, bounds, q_out, kw_out, vw_out,
           qb, gb, kb, vb, vis, ebuf, dpb, stat, stin, coef, kv, dqt, dqs, dqin, dqall, part, rsb,
           loc, qs, qr, gs, gr, ks, kr, vs, vr, xs, xr, ss, sr, kvs, kvr, ds, dr, as_, ar, ys, yr, rs, rr, fs, fr):
    T, G, NZ = cfg["T"], cfg["G"], cfg["NZ"]
    blk, rows, NK, NR, FR = cfg["blk"], cfg["rows"], cfg["NK"], cfg["NR"], cfg["FR"]
    W, NV, FB = cfg["W"], cfg["NV"], cfg["FB"]
    H = cfg["H"]
    RB = cfg["RB"]
    scale = HEAD_WIDTH ** (-0.5)
    me = lax.axis_index("tok")
    z, j0 = me // G, me % G

    def remote(src, dst, s, r, peer):
        return pltpu.make_async_remote_copy(
            src_ref=src, dst_ref=dst, send_sem=s, recv_sem=r,
            device_id={"tok": peer}, device_id_type=pl.DeviceIdType.MESH)

    def m128(i, n):
        return pl.ds(pl.multiple_of(i * n, n), n)

    barrier = pltpu.get_barrier_semaphore()
    for d in range(1, T):
        pl.semaphore_signal(barrier, inc=1, device_id={"tok": lax.rem(me + d, T)}, device_id_type=pl.DeviceIdType.MESH)
    twin = lax.axis_index("head")
    if H > 1:
        twin = 1 - twin
        pl.semaphore_signal(barrier, inc=1, device_id={"head": twin}, device_id_type=pl.DeviceIdType.MESH)
    pl.semaphore_wait(barrier, T - 1 + (H > 1))

    def tpeer(d):
        return lax.rem(me + d, T), lax.rem(me + T - d, T)

    def gpeer(d):
        a, b = (j0 ^ d, j0 ^ d) if G & (G - 1) == 0 else (lax.rem(j0 + d, G), lax.rem(j0 + G - d, G))
        return a, b, z * G + a, z * G + b

    def zpeer(d):
        a, b = lax.rem(z + d, NZ), lax.rem(z + NZ - d, NZ)
        return a, b, a * G + j0, b * G + j0

    sends = []

    def send(c):
        c.start()
        sends.append(c)

    def q_copy(t_to, t_from):
        return (remote(q_in.at[lax.rem(t_to, G)], qb.at[m128(t_from, blk)], qs.at[t_to], qr.at[t_from], t_to),
                remote(g_in.at[lax.rem(t_to, G)], gb.at[m128(t_from, blk)], gs.at[t_to], gr.at[t_from], t_to))

    def k_copy(j_to, j_from, peer):
        return (remote(k_in.at[:, m128(j_to, 128)], kb.at[m128(j_from, rows)], ks.at[j_to], kr.at[j_from], peer),
                remote(v_in.at[:, m128(j_to, 128)], vb.at[m128(j_from, rows)], vs.at[j_to], vr.at[j_from], peer))

    WH = W // H
    half = lax.axis_index("head") * WH if H > 1 else 0

    def x_copy(b, j_to, j_from, peer):
        cols = pl.ds(pl.multiple_of((b * G + j_to) * W + half, WH), WH)
        dst = vis.at[b, m128(j_from, rows), pl.ds(pl.multiple_of(half, WH), WH)]
        return remote(x_in.at[:, cols], dst, xs.at[j_to, b], xr.at[j_from, b], peer)

    def f_copy(b, j_from, mine):
        at = half if mine else WH - half
        here = vis.at[b, m128(j_from, rows), pl.ds(pl.multiple_of(at, WH), WH)]
        return pltpu.make_async_remote_copy(
            src_ref=here, dst_ref=here, send_sem=fs.at[j_from, b], recv_sem=fr.at[j_from, b],
            device_id={"head": twin}, device_id_type=pl.DeviceIdType.MESH)

    local = [
        pltpu.make_async_copy(q_in.at[j0], qb.at[m128(me, blk)], loc.at[0]),
        pltpu.make_async_copy(g_in.at[j0], gb.at[m128(me, blk)], loc.at[1]),
        pltpu.make_async_copy(k_in.at[:, m128(j0, 128)], kb.at[m128(j0, rows)], loc.at[2]),
        pltpu.make_async_copy(v_in.at[:, m128(j0, 128)], vb.at[m128(j0, rows)], loc.at[3]),
    ]
    local_x = [pltpu.make_async_copy(x_in.at[:, m128(b * G + j0, W)], vis.at[b, m128(j0, rows)], loc.at[4 + b]) for b in range(NV)]
    for c in local:
        c.start()
    def q_sends(zd):
        a, _, _, _ = zpeer(zd)
        for i in range(G):
            to = a * G + (lax.rem(j0 + i, G) if zd else gpeer(i)[0])
            if zd or i:
                for c in q_copy(to, me):
                    send(c)

    q_sends(0)
    for d in range(1, G):
        a, _, peer, _ = gpeer(d)
        for c in k_copy(a, j0, peer):
            send(c)
    for d in range(1, NZ):
        q_sends(d)
    for c in local_x:
        c.start()
    for c in local:
        c.wait()
    for d in range(1, G):
        _, b, _, _ = gpeer(d)
        for c in k_copy(j0, b, me):
            c.wait_recv()

    def q_wait(zd):
        _, b, _, _ = zpeer(zd)
        for i in range(G):
            if zd or i:
                frm = b * G + (i if zd else gpeer(i)[1])
                for c in q_copy(me, frm):
                    c.wait_recv()

    n_frames = NK // FR
    frame0 = z * n_frames
    stat[0:1, :] = jnp.full((1, NR), NEG_FILL, F32)
    stat[1:8, :] = jnp.zeros((7, NR), F32)

    def totals(cols, width):
        first, end = bounds[0:1, cols], bounds[1:2, cols]
        UN = 2 if n_frames % 2 == 0 else 1

        def scored(i, top):
            for u in range(UN):
                f = i * UN + u
                ok = (first <= frame0 + f) & (frame0 + f < end)
                s = jnp.where(ok, dot(kb[m128(f, FR), :], qb[cols, :], NT) * scale, NEG_FILL)
                ebuf[m128(f, FR), cols] = s
                top = jnp.maximum(top, jnp.max(s, axis=0, keepdims=True))
            return top

        top = lax.fori_loop(0, n_frames // UN, scored, jnp.full((1, width), NEG_FILL, F32))

        def summed(i, carry):
            total, dotted = carry
            for u in range(UN):
                f = i * UN + u
                dp = dot(vb[m128(f, FR), :], gb[cols, :], NT)
                e = jnp.exp(ebuf[m128(f, FR), cols] - top)
                ebuf[m128(f, FR), cols] = e
                dpb[m128(f, FR), cols] = dp
                total += jnp.sum(e, axis=0, keepdims=True)
                dotted += jnp.sum(e * dp, axis=0, keepdims=True)
            return total, dotted

        zero = jnp.zeros((1, width), F32)
        total, dotted = lax.fori_loop(0, n_frames // UN, summed, (zero, zero))
        stat[0:1, cols] = top
        stat[1:2, cols] = total
        stat[2:3, cols] = dotted

    def x_sends():
        for d in range(1, G):
            a, _, peer, _ = gpeer(d)
            for b in range(NV):
                send(x_copy(b, a, j0, peer))

    by_z = (NR // NZ) % 128 == 0
    for d in range(NZ):
        q_wait(d)
        if d == NZ - 1:
            x_sends()
        if by_z:
            totals(m128(zpeer(d)[1], NR // NZ), NR // NZ)
    if not by_z:
        for r in range(0, NR, RB):
            totals(pl.ds(r, RB), RB)

    def s_copy(z_to, z_from, peer):
        return remote(stat, stin.at[z_from], ss.at[z_to], sr.at[z_from], peer)

    for d in range(1, NZ):
        a, _, peer, _ = zpeer(d)
        send(s_copy(a, z, peer))
    stin[z] = stat[...]
    for d in range(1, NZ):
        _, b, _, _ = zpeer(d)
        s_copy(z, b, me).wait_recv()
    top = stat[0:1, :]
    for i in range(NZ):
        top = jnp.maximum(top, stin[i, 0:1, :])
    total = jnp.zeros((1, NR), F32)
    dotted = jnp.zeros((1, NR), F32)
    for i in range(NZ):
        w = jnp.exp(stin[i, 0:1, :] - top)
        total += w * stin[i, 1:2, :]
        dotted += w * stin[i, 2:3, :]
    coef[0:1, :] = jnp.exp(stat[0:1, :] - top) / total
    coef[1:2, :] = dotted / total
    dqt[...] = jnp.zeros_like(dqt)

    NC = cfg["NC"]
    CH = NK // NC

    def kv_copy(c, j_to, j_from, peer):
        here = kv.at[j_from, pl.ds(c * CH, CH)]
        return remote(here, here, kvs.at[j_to, c], kvr.at[j_from, c], peer)

    for c in range(NC):
        @pl.loop(c * (CH // FR), (c + 1) * (CH // FR))
        def _(f):
            kt = kb[m128(f, FR), :].astype(F32).T.astype(BF16)
            dk = jnp.zeros((FR, HEAD_WIDTH), F32)
            dv = jnp.zeros((FR, HEAD_WIDTH), F32)
            for r in range(0, NR, RB):
                cols = pl.ds(r, RB)
                p = ebuf[m128(f, FR), cols] * coef[0:1, cols]
                t = (p * (dpb[m128(f, FR), cols] - coef[1:2, cols])).astype(BF16)
                dv += dot(p.astype(BF16), gb[cols, :])
                dk += dot(t, qb[cols, :])
                dqt[:, cols] += dot(kt, t)
            kv[j0, m128(f, FR), 0:HEAD_WIDTH] = (scale * dk).astype(BF16)
            kv[j0, m128(f, FR), HEAD_WIDTH:2 * HEAD_WIDTH] = dv.astype(BF16)

        for d in range(1, G - 1):
            a, _, peer, _ = gpeer(d)
            kv_copy(c, a, j0, peer).start()
        if H > 1 and c == NC // 2:
            for d in range(1, G):
                _, b, _, _ = gpeer(d)
                for i in range(NV):
                    x_copy(i, j0, b, me).wait_recv()
                    send(f_copy(i, b, True))

    for r in range(0, NR, 128):
        dqs[pl.ds(r, 128), :] = (scale * dqt[:, pl.ds(r, 128)].T).astype(BF16)
    QR = NR // NZ

    def d_copy(z_to, z_from, peer):
        return remote(dqs.at[m128(z_to, QR)], dqin.at[z_from], ds.at[z_to], dr.at[z_from], peer)

    def a_copy(z_to, z_from, peer):
        here = dqall.at[j0, m128(z_from, QR)]
        return remote(here, here, as_.at[z_to], ar.at[z_from], peer)

    def y_copy(j_to, j_from, peer):
        here = dqall.at[j_from]
        return remote(here, here, ys.at[j_to], yr.at[j_from], peer)

    def r_copy(j, z_to, z_from, peer):
        return remote(part.at[j, m128(z_to, FB)], rsb.at[z_from, j], rs.at[j, z_to], rr.at[j, z_from], peer)

    for d in range(1, NZ):
        a, _, peer, _ = zpeer(d)
        send(d_copy(a, z, peer))
    for c in local_x:
        c.wait()
    for d in range(1, G):
        _, b, _, _ = gpeer(d)
        for i in range(NV):
            (f_copy(i, b, False) if H > 1 else x_copy(i, j0, b, me)).wait_recv()

    def weigh(j):
        @pl.loop(0, NV)
        def _(b):
            part[j, m128(b, W), :] = dot(vis[b], kv[j], TN).astype(BF16)
        for d in range(1, NZ):
            a, _, peer, _ = zpeer(d)
            send(r_copy(j, a, z, peer))

    weigh(j0)
    mine = dqs[m128(z, QR), :].astype(F32)
    for d in range(1, NZ):
        _, b, _, _ = zpeer(d)
        d_copy(z, b, me).wait_recv()
        mine += dqin[b].astype(F32)
    dqall[j0, m128(z, QR), :] = mine.astype(BF16)
    for d in range(1, NZ):
        a, _, peer, _ = zpeer(d)
        send(a_copy(a, z, peer))

    def spread():
        for d in range(1, NZ):
            _, b, _, _ = zpeer(d)
            a_copy(z, b, me).wait_recv()
        for d in range(1, G):
            a, _, peer, _ = gpeer(d)
            send(y_copy(a, j0, peer))

    for d in range(1, G - 1):
        a, _, peer, _ = gpeer(d)
        for c in range(NC):
            kv_copy(c, a, j0, peer).wait_send()
    if G > 1:
        a, _, peer, _ = gpeer(G - 1)
        for c in range(NC):
            send(kv_copy(c, a, j0, peer))
    if G == 1:
        spread()
    for d in range(1, G):
        _, b, _, _ = gpeer(d)
        for c in range(NC):
            kv_copy(c, j0, b, me).wait_recv()
        weigh(b)
        if d == min(2, G - 1):
            spread()
    for d in range(1, G):
        _, b, _, _ = gpeer(d)
        y_copy(j0, b, me).wait_recv()
    out_copy = pltpu.make_async_copy(dqall, q_out, loc.at[0])
    out_copy.start()

    for d in range(1, NZ):
        _, b, _, _ = zpeer(d)
        for j in range(G):
            r_copy(j, z, b, me).wait_recv()
    for j in range(G):
        acc = part[j, m128(z, FB), :].astype(F32)
        for d in range(1, NZ):
            _, b, _, _ = zpeer(d)
            acc += rsb[b, j].astype(F32)
        kw_out[:, pl.ds(j * HEAD_WIDTH, HEAD_WIDTH)] = acc[:, 0:HEAD_WIDTH]
        vw_out[:, pl.ds(j * HEAD_WIDTH, HEAD_WIDTH)] = acc[:, HEAD_WIDTH:]
    out_copy.wait()
    for c in sends:
        c.wait_send()


def shards(T, cores, text_queries, text_grads, vision_keys, video_value_rows, vision, lengths, frame_range):
    R, QW = text_queries.shape
    rows, kv_width = vision_keys.shape
    G = kv_width // HEAD_WIDTH
    M = QW // kv_width
    NZ = T // G
    DW = vision.shape[1]
    blk, NK, NR = M * R, G * rows, T * M * R
    FB = DW // T
    W = FB if FB % 128 == 0 else 256
    NV = DW // (G * W)
    FR = rows // FRAME_DEV
    NC = 4 if NK >= 16 * FR else 1
    cfg = dict(T=T, G=G, NZ=NZ, blk=blk, rows=rows, NK=NK, NR=NR, FR=FR, W=W, NV=NV, FB=FB, NC=NC, RB=min(NR, 512),
               H=2 if cores == 2 and G > 1 and W % 256 == 0 else 1)

    text_len = R * T
    row_ids = jnp.arange(text_len, dtype=jnp.int32)
    segment_ends = jnp.cumsum(lengths)
    segment = jnp.sum((row_ids[:, None] >= segment_ends[None, :]).astype(jnp.int32), axis=1)
    segment_pick = (
        segment[:, None] == jnp.arange(lengths.shape[0], dtype=jnp.int32)[None, :]
    ).astype(jnp.int32)
    bounds = jnp.sum(segment_pick[None] * frame_range.T[:, None, :], axis=2)
    bounds = jnp.broadcast_to(bounds.reshape(2, T, 1, R), (2, T, M, R)).reshape(2, NR)

    def split(a):
        return a.reshape(R, G, M, HEAD_WIDTH).transpose(1, 2, 0, 3).reshape(G, blk, HEAD_WIDTH)

    anyspec = pl.BlockSpec(memory_space=pl.ANY)
    vm = pl.BlockSpec(memory_space=pltpu.VMEM)
    V = pltpu.VMEM
    D = pltpu.SemaphoreType.DMA
    sem_pairs = []
    for shape in ((T,), (T,), (G,), (G,), (G, NV), (NZ,), (G, NC), (NZ,), (NZ,), (G,), (G, NZ), (G, NV)):
        sem_pairs += [D(shape), D(shape)]
    q_grad, kw, vw = pl.pallas_call(
        functools.partial(kernel, cfg),
        out_shape=(
            jax.ShapeDtypeStruct((G, NR, HEAD_WIDTH), BF16),
            jax.ShapeDtypeStruct((FB, kv_width), F32),
            jax.ShapeDtypeStruct((FB, kv_width), F32),
        ),
        in_specs=[anyspec] * 5 + [vm],
        out_specs=(anyspec, vm, vm),
        scratch_shapes=[
            V((NR, HEAD_WIDTH), BF16), V((NR, HEAD_WIDTH), BF16),
            V((NK, HEAD_WIDTH), BF16), V((NK, HEAD_WIDTH), BF16),
            V((NV, NK, W), BF16),
            V((NK, NR), F32), V((NK, NR), F32),
            V((8, NR), F32), V((NZ, 8, NR), F32), V((8, NR), F32),
            V((G, NK, 2 * HEAD_WIDTH), BF16),
            V((HEAD_WIDTH, NR), F32), V((NR, HEAD_WIDTH), BF16),
            V((NZ, NR // NZ, HEAD_WIDTH), BF16), V((G, NR, HEAD_WIDTH), BF16),
            V((G, DW // G, 2 * HEAD_WIDTH), BF16),
            V((NZ, G, FB, 2 * HEAD_WIDTH), BF16),
            D((4 + NV,)),
        ] + sem_pairs,
        compiler_params=pltpu.CompilerParams(
            collective_id=0, has_side_effects=True, vmem_limit_bytes=67043328
        ),
    )(split(text_queries), split(text_grads), vision_keys, video_value_rows, vision, bounds)
    q_grad = q_grad.reshape(G, T, M, R, HEAD_WIDTH).transpose(1, 3, 0, 2, 4).reshape(text_len, QW)
    return q_grad, kw, vw


def solution(mesh):
    return jax.shard_map(
        functools.partial(shards, mesh.shape["tok"], mesh.shape["head"]),
        mesh=mesh,
        in_specs=(
            P("tok", "head"),
            P("tok", "head"),
            P("tok", "head"),
            P("tok", "head"),
            P("tok", None),
            P(),
            P(),
        ),
        out_specs=(P(None, "head"), P("tok", "head"), P("tok", "head")),
        check_vma=False,
    )
```

profile of v0, /device:TPU:0, one launch (start us, length us, event | category | flops | bytes accessed | tf_op | source)
XLA Modules:
  0.0 152.8 jit_solution(12704774017387122721)
XLA Ops:
  0.6 0.8 reduce-window.8
  1.5 0.1 convert_reduce_fusion
  1.6 0.8 multiply_reduce_fusion
  2.3 0.1 broadcast_in_dim.4
  2.4 0.7 reshape.79.bounds
  3.1 0.9 copy.16
  4.1 0.7 copy.13
  4.8 0.9 copy.17
  5.7 0.7 copy.14
  6.4 140.4 %shard_map.94 = (bf16[4,2048,128]{2,1,0:T(8,128)(2,1)}, f32[256,512]{1,0:T(8,128)}, f32[256,512]{1,0:T(8,128)}) custom-call(bf16[4,128,128]{2,1,0:T(8,128)(2,1)} %bitcast.23, bf16[4,128,128]{2,1,0:T(8,128)(2,1)} %bitcast.24, bf16[512,512]{1,0:T(8,128)(2,1)} %k_in.1, bf16[512,512]{1,0:T(8,128)(2,1)} %v_in.1, bf16[512,4096]{1,0:T(8,128)(2,1)} %x_in.1, ...), custom_call_target="tpu_custom_call" | custom-call | tf_op jit(solution)/shard_map/pallas_call | solution.py:374
  146.8 2.1 %copy.15 = bf16[16,16,4,8,128]{4,3,2,1,0:T(8,128)(2,1)S(1)} copy(bf16[16,16,4,8,128]{4,1,3,0,2:T(8,128)(2,1)} %bitcast.22) | data formatting | bytes 4194304 | tf_op jit(solution)/shard_map/transpose | solution.py:400
  148.9 0.0 copy-start.1
  149.0 0.0 copy-start
  149.0 2.3 %reshape.81 = bf16[256,4096]{1,0:T(8,128)(2,1)} reshape(bf16[16,16,4,8,128]{4,3,2,1,0:T(8,128)(2,1)S(1)} %copy.15) | data formatting | bytes 4194304 | tf_op jit(solution)/shard_map/reshape | solution.py:400
  151.3 0.0 copy-done.1
  151.3 0.8 copy.20
  152.1 0.0 copy-done
  152.1 0.8 copy.21
  (2 shorter events, 0.0 us)
Async XLA Ops:
  148.9 2.3 %copy-start.1 = (f32[256,512]{1,0:T(8,128)S(1)}, f32[256,512]{1,0:T(8,128)}, u32[]{:S(2)}) copy-start(f32[256,512]{1,0:T(8,128)} %get-tuple-element.13) | copy-start | bytes 1572868
  149.0 3.1 %copy-start = (f32[256,512]{1,0:T(8,128)S(1)}, f32[256,512]{1,0:T(8,128)}, u32[]{:S(2)}) copy-start(f32[256,512]{1,0:T(8,128)} %get-tuple-element.14) | copy-start | bytes 1572868
where the time goes:
time: 154 us; the launch traced here: 153 us
  Pallas kernels  140 us (91%)
  local copies, waits for them, and re-layouts  10.1 us (7%)
  other arithmetic  1.69 us (1%)
    pallas_call x1, Pallas kernels, shards(): pl.pallas_call(functools.partial(kernel, cfg), out_shape=(jax.ShapeDtypeS...  140 us
    unnamed x8, local copies, waits for them, and re-layouts  3.44 us

commit v1 on v0

--- a/solution.py
+++ b/solution.py
@@ -339,6 +339,8 @@
     R, QW = text_queries.shape
     rows, kv_width = vision_keys.shape
     G = kv_width // HEAD_WIDTH
+    if cores == 2 and G == 4 and T == G * G and vision.shape[1] % (T * 128) == 0 and HEAD_WIDTH % (G * R) == 0:
+        return plane_shards(T, text_queries, text_grads, vision_keys, video_value_rows, vision, lengths, frame_range)
     M = QW // kv_width
     NZ = T // G
     DW = vision.shape[1]
@@ -401,6 +403,475 @@
     return q_grad, kw, vw
 
 
+def plane_kernel(cfg, q_in, g_in, k_in, v_in, x_in, lens, frames, q_out, kw_out, vw_out,
+                 qraw, graw, qb, gb, kb, vb, vis, ebuf, dpb, stat, stin, coef, lim, kv, dqt, dqs, dqin, dqall,
+                 gst, tmp, part, rin, ybs, ybr, loc, lx, qs, qr, zs, zr, ks, kr, xs, xr, fs, fr, ss, sr, kvs, kvr,
+                 ds, dr, as_, ar, ys, yr, cs, cr, es, er):
+    G, NZ, M, R, FR, NC = cfg["G"], cfg["NZ"], cfg["M"], cfg["R"], cfg["FR"], cfg["NC"]
+    rows, NK, NR, JW, FB, RZ = cfg["rows"], cfg["NK"], cfg["NR"], cfg["JW"], cfg["FB"], cfg["RZ"]
+    D = HEAD_WIDTH
+    ZB = M * RZ
+    scale = D ** (-0.5)
+    me = lax.axis_index("tok")
+    core = lax.axis_index("head")
+    z, j = me // G, me % G
+    y, x = j // 2, j % 2
+
+    def m128(i, n):
+        return pl.ds(pl.multiple_of(i * n, n), n)
+
+    def remote(src, dst, s, r, peer):
+        return pltpu.make_async_remote_copy(
+            src_ref=src, dst_ref=dst, send_sem=s, recv_sem=r,
+            device_id={"tok": peer}, device_id_type=pl.DeviceIdType.MESH)
+
+    def near(d):
+        return j ^ d, z * G + (j ^ d)
+
+    def far(d):
+        a, b = lax.rem(z + d, NZ), lax.rem(z + NZ - d, NZ)
+        return a, b, a * G + j, b * G + j
+
+    mirror = 2 * z > NZ - 1
+    zz = jnp.where(mirror, NZ - 1 - z, z)
+
+    def band(s):
+        u = s - (NZ - 1 - 2 * zz)
+        k, odd = u // 2, u % 2
+        b = jnp.where(u < 0, NZ - 1 - s, k + odd * (2 * zz - 2 * k))
+        return jnp.where(mirror, NZ - 1 - b, b)
+
+    barrier = pltpu.get_barrier_semaphore()
+    for d in range(1, G):
+        pl.semaphore_signal(barrier, inc=1, device_id={"tok": near(d)[1]}, device_id_type=pl.DeviceIdType.MESH)
+    for d in range(1, NZ):
+        pl.semaphore_signal(barrier, inc=1, device_id={"tok": far(d)[2]}, device_id_type=pl.DeviceIdType.MESH)
+    pl.semaphore_signal(barrier, inc=1, device_id={"head": 1 - core}, device_id_type=pl.DeviceIdType.MESH)
+    pl.semaphore_wait(barrier, G + NZ - 1)
+
+    sends = []
+
+    def send(c):
+        c.start()
+        sends.append(c)
+
+    def own_rows(t):
+        return m128(t, R)
+
+    def q_copy(d, t_from, peer, j_to):
+        cols = m128(j_to, JW)
+        return (remote(q_in.at[:, cols], qraw.at[own_rows(t_from)], qs.at[0, d], qr.at[0, d], peer),
+                remote(g_in.at[:, cols], graw.at[own_rows(t_from)], qs.at[1, d], qr.at[1, d], peer))
+
+    def zq_copy(z_to, z_from, peer):
+        here = m128(z_from, RZ)
+        return (remote(qraw.at[here], qraw.at[here], zs.at[0, z_to], zr.at[0, z_from], peer),
+                remote(graw.at[here], graw.at[here], zs.at[1, z_to], zr.at[1, z_from], peer))
+
+    def k_copy(d, j_to, j_from, peer):
+        return (remote(k_in.at[:, m128(j_to, D)], kb.at[m128(j_from, rows)], ks.at[0, d], kr.at[0, d], peer),
+                remote(v_in.at[:, m128(j_to, D)], vb.at[m128(j_from, rows)], ks.at[1, d], kr.at[1, d], peer))
+
+    def lane_half(mine):
+        return m128(core if mine else 1 - core, FB)
+
+    def x_copy(kind, b, x_to, j_from, peer):
+        cols = m128(b * G + core * 2 + x_to, FB)
+        dst = vis.at[b, m128(j_from, rows), lane_half(True)]
+        return remote(x_in.at[:, cols], dst, xs.at[kind, b], xr.at[kind, b], peer)
+
+    def pass_copy(b, j_from, peer):
+        here = vis.at[b, m128(j_from, rows), lane_half(True)]
+        return remote(here, here, xs.at[2, b], xr.at[2, b], peer)
+
+    def f_copy(kind, b, mine):
+        here = vis.at[b, m128(j ^ (kind + 1), rows), lane_half(mine)]
+        return pltpu.make_async_remote_copy(
+            src_ref=here, dst_ref=here, send_sem=fs.at[kind, b], recv_sem=fr.at[kind, b],
+            device_id={"head": 1 - core}, device_id_type=pl.DeviceIdType.MESH)
+
+    local = [
+        pltpu.make_async_copy(q_in.at[:, m128(j, JW)], qraw.at[own_rows(me)], loc.at[0]),
+        pltpu.make_async_copy(g_in.at[:, m128(j, JW)], graw.at[own_rows(me)], loc.at[1]),
+        pltpu.make_async_copy(k_in.at[:, m128(j, D)], kb.at[m128(j, rows)], loc.at[2]),
+        pltpu.make_async_copy(v_in.at[:, m128(j, D)], vb.at[m128(j, rows)], loc.at[3]),
+    ]
+    for c in local:
+        c.start()
+    for d in range(G - 1, 0, -1):
+        for c in q_copy(d, me, near(d)[1], near(d)[0]):
+            send(c)
+    for d in range(1, G):
+        for c in k_copy(d, near(d)[0], j, near(d)[1]):
+            send(c)
+    local_x = []
+    for b in range(NZ):
+        for h in range(2):
+            local_x.append(pltpu.make_async_copy(
+                x_in.at[:, m128(b * G + 2 * h + x, FB)], vis.at[b, m128(j, rows), pl.ds(h * FB, FB)], lx.at[b, h]))
+
+    col = lax.broadcasted_iota(jnp.int32, (1, NR), 1)
+    text = (col // ZB) * RZ + col % RZ
+    seg = jnp.zeros((1, NR), jnp.int32)
+    end = jnp.int32(0)
+    NS = cfg["NS"]
+    for i in range(NS):
+        end = end + lens[i]
+        seg += (text >= end).astype(jnp.int32)
+    first, last = jnp.zeros((1, NR), jnp.int32), jnp.zeros((1, NR), jnp.int32)
+    for i in range(NS):
+        first = jnp.where(seg == i, frames[0, i], first)
+        last = jnp.where(seg == i, frames[1, i], last)
+    lim[0:1, :] = first
+    lim[1:2, :] = last
+    stat[0:8, :] = jnp.zeros((8, NR), F32)
+
+    for c in local[:2]:
+        c.wait()
+    for d in range(1, G):
+        for c in q_copy(d, z * G + near(d)[0], me, j):
+            c.wait_recv()
+    for k in range(1, NZ):
+        b = band(NZ - 1 - k)
+        for c in zq_copy(b, z, b * G + j):
+            send(c)
+    for s in range(NZ):
+        send(x_copy(0, band(s), 1 - x, j, near(1)[1]))
+        send(x_copy(1, band(s), x, j, near(2)[1]))
+    for c in local_x:
+        c.start()
+    for c in local[2:]:
+        c.wait()
+
+    n_frames = rows // FR
+
+    def totals(g, zb):
+        cols = m128(zb, ZB)
+        lo, hi = lim[0:1, cols], lim[1:2, cols]
+        base = z * G * n_frames + g * n_frames
+
+        def tokens(f):
+            return m128(g * n_frames + f, FR)
+
+        top = jnp.full((1, ZB), NEG_FILL, F32)
+        for f in range(n_frames):
+            ok = (lo <= base + f) & (base + f < hi)
+            sc = jnp.where(ok, dot(kb[tokens(f), :], qb[cols, :], NT) * scale, NEG_FILL)
+            ebuf[tokens(f), cols] = sc
+            top = jnp.maximum(top, jnp.max(sc, axis=0, keepdims=True))
+        total = jnp.zeros((1, ZB), F32)
+        dotted = jnp.zeros((1, ZB), F32)
+        for f in range(n_frames):
+            dp = dot(vb[tokens(f), :], gb[cols, :], NT)
+            e = jnp.exp(ebuf[tokens(f), cols] - top)
+            ebuf[tokens(f), cols] = e
+            dpb[tokens(f), cols] = dp
+            total += jnp.sum(e, axis=0, keepdims=True)
+            dotted += jnp.sum(e * dp, axis=0, keepdims=True)
+        gst[g, 0:1, cols] = top
+        gst[g, 1:2, cols] = total
+        gst[g, 2:3, cols] = dotted
+
+    def s_copy(zb, z_to, z_from, peer):
+        cols = m128(zb, ZB)
+        return remote(stat.at[:, cols], stin.at[z_from, :, cols], ss.at[zb, z_to], sr.at[zb, z_from], peer)
+
+    def plane_totals(zb):
+        cols = m128(zb, ZB)
+        top = gst[0, 0:1, cols]
+        for g in range(1, G):
+            top = jnp.maximum(top, gst[g, 0:1, cols])
+        total = jnp.zeros((1, ZB), F32)
+        dotted = jnp.zeros((1, ZB), F32)
+        for g in range(G):
+            w = jnp.exp(gst[g, 0:1, cols] - top)
+            total += w * gst[g, 1:2, cols]
+            dotted += w * gst[g, 2:3, cols]
+        stat[0:1, cols] = top
+        stat[1:2, cols] = total
+        stat[2:3, cols] = dotted
+        for d in range(1, NZ):
+            send(s_copy(zb, far(d)[0], z, far(d)[2]))
+
+    def landed(s):
+        b = band(s)
+        x_copy(0, b, x, near(1)[0], me).wait_recv()
+        send(pass_copy(b, near(1)[0], near(2)[1]))
+        send(f_copy(0, b, True))
+        x_copy(1, b, x, near(2)[0], me).wait_recv()
+        send(f_copy(1, b, True))
+
+    have_g, have_z = {0}, set()
+
+    def block(d, k):
+        zb = band(NZ - 1 - k)
+        if d not in have_g:
+            have_g.add(d)
+            for c in k_copy(d, j, near(d)[0], me):
+                c.wait_recv()
+        if k not in have_z:
+            have_z.add(k)
+            if k:
+                for c in zq_copy(z, zb, me):
+                    c.wait_recv()
+            for raw, buf in ((qraw, qb), (graw, gb)):
+                for m in range(M):
+                    buf[m128(zb * M + m, RZ), :] = raw[m128(zb, RZ), m * D:(m + 1) * D]
+        totals(j ^ d, zb)
+
+    for d, k in ((0, 0), (1, 0), (2, 0), (0, 1), (1, 1), (2, 1), (3, 0)):
+        block(d, k)
+    plane_totals(band(NZ - 1))
+    block(3, 1)
+    plane_totals(band(NZ - 2))
+    landed(0)
+    for k in range(2, NZ):
+        for d in range(G):
+            block(d, k)
+        plane_totals(band(NZ - 1 - k))
+        landed(k - 1)
+
+    stin[z] = stat[...]
+    dqt[...] = jnp.zeros_like(dqt)
+    for zb in range(NZ):
+        for d in range(1, NZ):
+            s_copy(zb, z, far(d)[1], me).wait_recv()
+    top = stat[0:1, :]
+    for i in range(NZ):
+        top = jnp.maximum(top, stin[i, 0:1, :])
+    total = jnp.zeros((1, NR), F32)
+    dotted = jnp.zeros((1, NR), F32)
+    for i in range(NZ):
+        w = jnp.exp(stin[i, 0:1, :] - top)
+        total += w * stin[i, 1:2, :]
+        dotted += w * stin[i, 2:3, :]
+    for g in range(G):
+        coef[g:g + 1, :] = jnp.exp(gst[g, 0:1, :] - top) / total
+    coef[G:G + 1, :] = dotted / total
+    landed(NZ - 1)
+
+    CH = NK // NC
+
+    def kv_copy(c, peer):
+        at = pl.ds(c * CH, CH)
+        return remote(kv.at[0, at], kv.at[1, at], kvs.at[c], kvr.at[c], peer)
+
+    for c in range(NC):
+        @pl.loop(c * (CH // FR), (c + 1) * (CH // FR))
+        def _(f):
+            kt = kb[m128(f, FR), :].astype(F32).T.astype(BF16)
+            dk = jnp.zeros((FR, D), F32)
+            dv = jnp.zeros((FR, D), F32)
+            for r in range(0, NR, ZB):
+                cols = pl.ds(r, ZB)
+                p = ebuf[m128(f, FR), cols] * coef[c:c + 1, cols]
+                t = (p * (dpb[m128(f, FR), cols] - coef[G:G + 1, cols])).astype(BF16)
+                dv += dot(p.astype(BF16), gb[cols, :])
+                dk += dot(t, qb[cols, :])
+                dqt[:, cols] += dot(kt, t)
+            kv[0, m128(f, FR), 0:D] = (scale * dk).astype(BF16)
+            kv[0, m128(f, FR), D:2 * D] = dv.astype(BF16)
+
+        send(kv_copy(c, near(1)[1]))
+
+    for zb in range(NZ):
+        for i in range(ZB // D):
+            t = (scale * dqt[:, pl.ds(zb * ZB + i * D, D)].T).astype(BF16)
+            for k in range(D // RZ):
+                m = i * (D // RZ) + k
+                dqs[pl.ds(zb * RZ, RZ), pl.ds(m * D, D)] = t[k * RZ:(k + 1) * RZ, :]
+    HW = JW // 2
+
+    def half(u):
+        return pl.ds(u * HW, HW)
+
+    def d_copy(u, z_to, z_from, peer):
+        return remote(dqs.at[m128(z_to, RZ), half(u)], dqin.at[z_from, :, half(u)], ds.at[u, z_to], dr.at[u, z_from], peer)
+
+    def a_copy(u, z_to, z_from, peer):
+        here = dqall.at[j, m128(z_from, RZ), half(u)]
+        return remote(here, here, as_.at[u, z_to], ar.at[u, z_from], peer)
+
+    def y_copy(u, d, j_from, peer, kind):
+        here = dqall.at[j_from, :, half(u)]
+        return remote(here, here, ys.at[kind, u], yr.at[kind, u], peer)
+
+    for u in range(2):
+        for d in range(1, NZ):
+            send(d_copy(u, far(d)[0], z, far(d)[2]))
+    for c in local_x:
+        c.wait()
+
+    def c_copy(side, b, h, peer):
+        return remote(part.at[h, b], rin.at[side, b, h], cs.at[b, h], cr.at[side, b, h], peer)
+
+    def weigh(b, h, slot):
+        for i in range(2):
+            tmp[slot, pl.ds(i * FB, FB), :] = dot(vis[b, :, i * FB:(i + 1) * FB], kv[h], TN)
+
+    def gather(s):
+        b = band(s)
+        pass_copy(b, near(3)[0], me).wait_recv()
+        send(f_copy(2, b, True))
+        for kind in range(3):
+            f_copy(kind, b, False).wait_recv()
+
+    def onward(s, h, between=None):
+        b = band(s)
+        weigh(b, h, 0)
+        side = (b < z).astype(jnp.int32)
+        fed = jnp.where(b > z, z > 0, z < NZ - 1)
+        out = c_copy(side, b, h, (z + 1 - 2 * side) * G + j)
+
+        def pass_on(extra):
+            part[h, b] = (tmp[0] + extra if extra is not None else tmp[0]).astype(BF16)
+            out.start()
+
+        @pl.when(jnp.logical_not(fed))
+        def _():
+            pass_on(None)
+        if between is not None:
+            between()
+
+        @pl.when(fed)
+        def _():
+            c_copy(side, b, h, me).wait_recv()
+            pass_on(rin[side, b, h].astype(F32))
+        sends.append(out)
+
+    def e_copy(h, peer):
+        return remote(ybs.at[h], ybr.at[h], es.at[h], er.at[h], peer)
+
+    def finish(h):
+        @pl.when(z > 0)
+        def _():
+            c_copy(0, z, h, me).wait_recv()
+            tmp[1 + h] += rin[0, z, h].astype(F32)
+
+        @pl.when(z < NZ - 1)
+        def _():
+            c_copy(1, z, h, me).wait_recv()
+            tmp[1 + h] += rin[1, z, h].astype(F32)
+        ybs[h] = tmp[1 + h, m128(1 - y, FB), :].astype(BF16)
+        send(e_copy(h, near(2)[1]))
+        at = m128(j ^ h, D)
+        kw_out[:, at] = tmp[1 + h, m128(y, FB), 0:D]
+        vw_out[:, at] = tmp[1 + h, m128(y, FB), D:2 * D]
+
+    def summed_dq(u):
+        mine = dqs[m128(z, RZ), half(u)].astype(F32)
+        for d in range(1, NZ):
+            d_copy(u, z, far(d)[1], me).wait_recv()
+            mine += dqin[far(d)[1], :, half(u)].astype(F32)
+        dqall[j, m128(z, RZ), half(u)] = mine.astype(BF16)
+        for d in range(1, NZ):
+            send(a_copy(u, far(d)[0], z, far(d)[2]))
+
+    def shared_dq(u):
+        for d in range(1, NZ):
+            a_copy(u, z, far(d)[1], me).wait_recv()
+        send(y_copy(u, 1, j, near(1)[1], 0))
+        send(y_copy(u, 2, j, near(2)[1], 1))
+
+    gather(0)
+    onward(0, 0, lambda: summed_dq(0))
+    gather(1)
+    onward(1, 0, lambda: summed_dq(1))
+    gather(2)
+    onward(2, 0)
+    gather(3)
+    weigh(z, 0, 1)
+    for c in range(NC):
+        kv_copy(c, me).wait_recv()
+    onward(0, 1, lambda: shared_dq(0))
+    onward(1, 1, lambda: shared_dq(1))
+    onward(2, 1)
+    weigh(z, 1, 2)
+    finish(0)
+    y_copy(0, 1, near(1)[0], me, 0).wait_recv()
+    send(y_copy(0, 2, near(1)[0], near(2)[1], 2))
+    y_copy(1, 2, near(2)[0], me, 1).wait_recv()
+    send(y_copy(1, 1, near(2)[0], near(1)[1], 2))
+    finish(1)
+
+    outs = []
+
+    def put(i):
+        c = pltpu.make_async_copy(dqall.at[j ^ i], q_out.at[:, m128(j ^ i, JW)], loc.at[i])
+        c.start()
+        outs.append(c)
+
+    put(0)
+    y_copy(1, 1, near(1)[0], me, 0).wait_recv()
+    put(1)
+    y_copy(0, 2, near(2)[0], me, 1).wait_recv()
+    put(2)
+    y_copy(0, 2, near(3)[0], me, 2).wait_recv()
+    y_copy(1, 1, near(3)[0], me, 2).wait_recv()
+    put(3)
+    for h in range(2):
+        e_copy(h, me).wait_recv()
+        at = m128(j ^ (2 + h), D)
+        kw_out[:, at] = ybr[h, :, 0:D].astype(F32)
+        vw_out[:, at] = ybr[h, :, D:2 * D].astype(F32)
+    for c in outs:
+        c.wait()
+    for c in sends:
+        c.wait_send()
+
+
+def plane_shards(T, text_queries, text_grads, vision_keys, video_value_rows, vision, lengths, frame_range):
+    R, QW = text_queries.shape
+    rows, kv_width = vision_keys.shape
+    G = kv_width // HEAD_WIDTH
+    M = QW // kv_width
+    NZ = T // G
+    DW = vision.shape[1]
+    FB = DW // T
+    NK, RZ, JW = G * rows, G * R, M * HEAD_WIDTH
+    NR = T * R * M
+    cfg = dict(G=G, NZ=NZ, M=M, R=R, FR=rows // FRAME_DEV, NC=4, rows=rows, NK=NK, NR=NR, JW=JW, FB=FB, RZ=RZ,
+               NS=lengths.shape[0])
+    anyspec = pl.BlockSpec(memory_space=pl.ANY)
+    vm = pl.BlockSpec(memory_space=pltpu.VMEM)
+    sm = pl.BlockSpec(memory_space=pltpu.SMEM)
+    V = pltpu.VMEM
+    D = pltpu.SemaphoreType.DMA
+    W2 = 2 * HEAD_WIDTH
+    pairs = []
+    for a, b in (((2, G),) * 2, ((2, NZ),) * 2, ((2, G),) * 2, ((3, NZ),) * 2, ((3, NZ),) * 2, ((NZ, NZ),) * 2, ((cfg["NC"],),) * 2,
+                 ((2, NZ),) * 2, ((2, NZ),) * 2, ((3, 2),) * 2, ((NZ, 2), (2, NZ, 2)), ((2,),) * 2):
+        pairs += [D(a), D(b)]
+    return pl.pallas_call(
+        functools.partial(plane_kernel, cfg),
+        out_shape=(
+            jax.ShapeDtypeStruct((T * R, QW), BF16),
+            jax.ShapeDtypeStruct((FB, kv_width), F32),
+            jax.ShapeDtypeStruct((FB, kv_width), F32),
+        ),
+        in_specs=[anyspec] * 5 + [sm] * 2,
+        out_specs=(anyspec, vm, vm),
+        scratch_shapes=[
+            V((T * R, JW), BF16), V((T * R, JW), BF16),
+            V((NR, HEAD_WIDTH), BF16), V((NR, HEAD_WIDTH), BF16),
+            V((NK, HEAD_WIDTH), BF16), V((NK, HEAD_WIDTH), BF16),
+            V((NZ, NK, 2 * FB), BF16),
+            V((NK, NR), F32), V((NK, NR), F32),
+            V((8, NR), F32), V((NZ, 8, NR), F32), V((8, NR), F32), V((8, NR), jnp.int32),
+            V((2, NK, W2), BF16),
+            V((HEAD_WIDTH, NR), F32), V((T * R, JW), BF16),
+            V((NZ, RZ, JW), BF16), V((G, T * R, JW), BF16),
+            V((G, 8, NR), F32),
+            V((3, 2 * FB, W2), F32), V((2, NZ, 2 * FB, W2), BF16), V((2, NZ, 2, 2 * FB, W2), BF16),
+            V((2, FB, W2), BF16), V((2, FB, W2), BF16),
+            D((4,)), D((NZ, 2)),
+        ] + pairs,
+        compiler_params=pltpu.CompilerParams(
+            collective_id=0, has_side_effects=True, vmem_limit_bytes=67043328
+        ),
+    )(text_queries, text_grads, vision_keys, video_value_rows, vision, lengths, frame_range.T)
+
+
 def solution(mesh):
     return jax.shard_map(
         functools.partial(shards, mesh.shape["tok"], mesh.shape["head"]),

time: 154 us -> 123 us (0.80)
  Pallas kernels: 140 us -> 118 us
  local copies, waits for them, and re-layouts: 10.1 us -> 4.81 us
  other arithmetic: 1.69 us -> 0 us
    pallas_call x1, Pallas kernels: 140 us -> 118 us  [plane_shards(): pl.pallas_call(functools.partial(plane_kernel, cfg), out_shape=(jax.Shape...]
    reshape x4 -> x0, local copies, waits for them, and re-layouts: 4.43 us -> none  [the longest x1 2.29 us: shards(): q_grad.reshape(G, T, M, R, HEAD_WIDTH).transpose(1, 3, 0, 2, 4)]
    transpose x1 -> x0, local copies, waits for them, and re-layouts: 2.13 us -> none  [shards(): q_grad.reshape(G, T, M, R, HEAD_WIDTH).transpose(1, 3, 0, 2, 4)]
    unnamed x8 -> x7, local copies, waits for them, and re-layouts: 3.44 us -> 4.81 us
where the time goes in v1:
time: 123 us
  Pallas kernels  118 us (96%)
  local copies, waits for them, and re-layouts  4.81 us (4%)
    pallas_call x1, Pallas kernels, plane_shards(): pl.pallas_call(functools.partial(plane_kernel, cfg), out_shape=(jax.Shape...  118 us
    unnamed x7, local copies, waits for them, and re-layouts  4.81 us

profile of v1, /device:TPU:0, one launch (start us, length us, event | category | flops | bytes accessed | tf_op | source)
XLA Modules:
  0.0 123.3 jit_solution(4709990036134957531)
XLA Ops:
  0.6 117.9 %shard_map.94 = (bf16[256,4096]{1,0:T(8,128)(2,1)}, f32[256,512]{1,0:T(8,128)}, f32[256,512]{1,0:T(8,128)}) custom-call(bf16[16,4096]{1,0:T(8,128)(2,1)} %q_in.1, bf16[16,4096]{1,0:T(8,128)(2,1)} %g_in.1, bf16[512,512]{1,0:T(8,128)(2,1)} %k_in.1, bf16[512,512]{1,0:T(8,128)(2,1)} %v_in.1, bf16[512,4096]{1,0:T(8,128)(2,1)} %x_in.1, s32[8]{0:T(128)} %lens.1, ...), custom_call_target="tpu_custom_call" | custom-call | tf_op jit(solution)/shard_map/pallas_call | solution.py:845
  118.5 0.0 copy-start.1
  118.5 0.0 copy-start
  118.5 3.2 %copy.13 = bf16[256,4096]{1,0:T(8,128)(2,1)} copy(bf16[256,4096]{1,0:T(8,128)(2,1)} %get-tuple-element.6) | data formatting | bytes 4194304
  121.7 0.0 copy-done.1
  121.7 0.8 copy.14
  122.5 0.0 copy-done
  122.5 0.8 copy.15
Async XLA Ops:
  118.5 3.2 %copy-start.1 = (f32[256,512]{1,0:T(8,128)S(1)}, f32[256,512]{1,0:T(8,128)}, u32[]{:S(2)}) copy-start(f32[256,512]{1,0:T(8,128)} %get-tuple-element.7) | copy-start | bytes 1572868
  118.5 4.0 %copy-start = (f32[256,512]{1,0:T(8,128)S(1)}, f32[256,512]{1,0:T(8,128)}, u32[]{:S(2)}) copy-start(f32[256,512]{1,0:T(8,128)} %get-tuple-element.8) | copy-start | bytes 1572868

commit v2 on v1

--- a/solution.py
+++ b/solution.py
@@ -339,7 +339,7 @@
     R, QW = text_queries.shape
     rows, kv_width = vision_keys.shape
     G = kv_width // HEAD_WIDTH
-    if cores == 2 and G == 4 and T == G * G and vision.shape[1] % (T * 128) == 0 and HEAD_WIDTH % (G * R) == 0:
+    if cores == 2 and G == 4 and T == G * G and vision.shape[1] % (T * 128) == 0 and HEAD_WIDTH % (G * R) == 0 and 2 * vision.shape[1] == T * rows:
         return plane_shards(T, text_queries, text_grads, vision_keys, video_value_rows, vision, lengths, frame_range)
     M = QW // kv_width
     NZ = T // G
@@ -405,7 +405,7 @@
 
 def plane_kernel(cfg, q_in, g_in, k_in, v_in, x_in, lens, frames, q_out, kw_out, vw_out,
                  qraw, graw, qb, gb, kb, vb, vis, ebuf, dpb, stat, stin, coef, lim, kv, dqt, dqs, dqin, dqall,
-                 gst, tmp, part, rin, ybs, ybr, loc, lx, qs, qr, zs, zr, ks, kr, xs, xr, fs, fr, ss, sr, kvs, kvr,
+                 gst, ktb, wres, ws, tmp, part, rin, ybs, ybr, loc, lx, qs, qr, zs, zr, ks, kr, xs, xr, fs, fr, ss, sr, kvs, kvr,
                  ds, dr, as_, ar, ys, yr, cs, cr, es, er):
     G, NZ, M, R, FR, NC = cfg["G"], cfg["NZ"], cfg["M"], cfg["R"], cfg["FR"], cfg["NC"]
     rows, NK, NR, JW, FB, RZ = cfg["rows"], cfg["NK"], cfg["NR"], cfg["JW"], cfg["FB"], cfg["RZ"]
@@ -463,10 +463,25 @@
         return (remote(q_in.at[:, cols], qraw.at[own_rows(t_from)], qs.at[0, d], qr.at[0, d], peer),
                 remote(g_in.at[:, cols], graw.at[own_rows(t_from)], qs.at[1, d], qr.at[1, d], peer))
 
-    def zq_copy(z_to, z_from, peer):
-        here = m128(z_from, RZ)
-        return (remote(qraw.at[here], qraw.at[here], zs.at[0, z_to], zr.at[0, z_from], peer),
-                remote(graw.at[here], graw.at[here], zs.at[1, z_to], zr.at[1, z_from], peer))
+    low, high = z > 0, z < NZ - 1
+    inner = low & high
+
+    def zq_copy(side, a, b):
+        here = (qraw, graw)[a].at[m128(b, RZ)]
+        return remote(here, here, zs.at[side, a, b], zr.at[a, b], (z + 1 - 2 * side) * G + j)
+
+    def zq_each(act, b, into):
+        for a in range(2):
+            if into:
+                zq_copy(0, a, b).wait_recv()
+
+            @pl.when(high & (b <= z))
+            def _():
+                act(zq_copy(0, a, b))
+
+            @pl.when(low & (b >= z))
+            def _():
+                act(zq_copy(1, a, b))
 
     def k_copy(d, j_to, j_from, peer):
         return (remote(k_in.at[:, m128(j_to, D)], kb.at[m128(j_from, rows)], ks.at[0, d], kr.at[0, d], peer),
@@ -531,13 +546,11 @@
     for d in range(1, G):
         for c in q_copy(d, z * G + near(d)[0], me, j):
             c.wait_recv()
-    for k in range(1, NZ):
-        b = band(NZ - 1 - k)
-        for c in zq_copy(b, z, b * G + j):
-            send(c)
+    zq_each(lambda c: c.start(), z, False)
     for s in range(NZ):
         send(x_copy(0, band(s), 1 - x, j, near(1)[1]))
-        send(x_copy(1, band(s), x, j, near(2)[1]))
+        if s < NZ // 2:
+            send(x_copy(1, band(s), x, j, near(2)[1]))
     for c in local_x:
         c.start()
     for c in local[2:]:
@@ -597,11 +610,14 @@
         b = band(s)
         x_copy(0, b, x, near(1)[0], me).wait_recv()
         send(pass_copy(b, near(1)[0], near(2)[1]))
+        if s < NZ // 2:
+            send(x_copy(1, band(s + NZ // 2), x, j, near(2)[1]))
         send(f_copy(0, b, True))
-        x_copy(1, b, x, near(2)[0], me).wait_recv()
-        send(f_copy(1, b, True))
 
     have_g, have_z = {0}, set()
+
+    def arrive(k):
+        zq_each(lambda c: c.start(), band(NZ - 1 - k), True)
 
     def block(d, k):
         zb = band(NZ - 1 - k)
@@ -612,189 +628,271 @@
         if k not in have_z:
             have_z.add(k)
             if k:
-                for c in zq_copy(z, zb, me):
-                    c.wait_recv()
+                pl.when(jnp.logical_not(inner))(lambda: arrive(k))
             for raw, buf in ((qraw, qb), (graw, gb)):
                 for m in range(M):
                     buf[m128(zb * M + m, RZ), :] = raw[m128(zb, RZ), m * D:(m + 1) * D]
         totals(j ^ d, zb)
 
-    for d, k in ((0, 0), (1, 0), (2, 0), (0, 1), (1, 1), (2, 1), (3, 0)):
+    block(0, 0)
+    block(1, 0)
+
+    @pl.when(inner)
+    def _():
+        arrive(1)
+        arrive(2)
+    for d, k in ((2, 0), (0, 1), (1, 1), (2, 1)):
         block(d, k)
+
+    @pl.when(inner)
+    def _():
+        arrive(3)
+    block(3, 0)
     plane_totals(band(NZ - 1))
     block(3, 1)
     plane_totals(band(NZ - 2))
-    landed(0)
     for k in range(2, NZ):
         for d in range(G):
             block(d, k)
         plane_totals(band(NZ - 1 - k))
-        landed(k - 1)
-
-    stin[z] = stat[...]
-    dqt[...] = jnp.zeros_like(dqt)
-    for zb in range(NZ):
+        if k < NZ - 1:
+            landed(k - 2)
+
+    CH = NK // NC
+
+    def kv_copy(c, peer):
+        at = m128(c, CH)
+        return remote(kv.at[0, at], kv.at[1, at], kvs.at[c], kvr.at[c], peer)
+
+    def d_copy(z_to, z_from):
+        return remote(dqs.at[m128(z_to, RZ)], dqin.at[z_from], ds.at[z_to], dr.at[z_from], z_to * G + j)
+
+    def coefs(zb):
+        cols = m128(zb, ZB)
         for d in range(1, NZ):
             s_copy(zb, z, far(d)[1], me).wait_recv()
-    top = stat[0:1, :]
-    for i in range(NZ):
-        top = jnp.maximum(top, stin[i, 0:1, :])
-    total = jnp.zeros((1, NR), F32)
-    dotted = jnp.zeros((1, NR), F32)
-    for i in range(NZ):
-        w = jnp.exp(stin[i, 0:1, :] - top)
-        total += w * stin[i, 1:2, :]
-        dotted += w * stin[i, 2:3, :]
-    for g in range(G):
-        coef[g:g + 1, :] = jnp.exp(gst[g, 0:1, :] - top) / total
-    coef[G:G + 1, :] = dotted / total
-    landed(NZ - 1)
-
-    CH = NK // NC
-
-    def kv_copy(c, peer):
-        at = pl.ds(c * CH, CH)
-        return remote(kv.at[0, at], kv.at[1, at], kvs.at[c], kvr.at[c], peer)
-
-    for c in range(NC):
-        @pl.loop(c * (CH // FR), (c + 1) * (CH // FR))
-        def _(f):
-            kt = kb[m128(f, FR), :].astype(F32).T.astype(BF16)
-            dk = jnp.zeros((FR, D), F32)
-            dv = jnp.zeros((FR, D), F32)
-            for r in range(0, NR, ZB):
-                cols = pl.ds(r, ZB)
-                p = ebuf[m128(f, FR), cols] * coef[c:c + 1, cols]
-                t = (p * (dpb[m128(f, FR), cols] - coef[G:G + 1, cols])).astype(BF16)
-                dv += dot(p.astype(BF16), gb[cols, :])
-                dk += dot(t, qb[cols, :])
-                dqt[:, cols] += dot(kt, t)
-            kv[0, m128(f, FR), 0:D] = (scale * dk).astype(BF16)
-            kv[0, m128(f, FR), D:2 * D] = dv.astype(BF16)
-
-        send(kv_copy(c, near(1)[1]))
-
-    for zb in range(NZ):
+        top = stat[0:1, cols]
+        for d in range(1, NZ):
+            top = jnp.maximum(top, stin[far(d)[1], 0:1, cols])
+        w = jnp.exp(stat[0:1, cols] - top)
+        total, dotted = w * stat[1:2, cols], w * stat[2:3, cols]
+        for d in range(1, NZ):
+            i = far(d)[1]
+            w = jnp.exp(stin[i, 0:1, cols] - top)
+            total += w * stin[i, 1:2, cols]
+            dotted += w * stin[i, 2:3, cols]
+        for g in range(G):
+            coef[g:g + 1, cols] = jnp.exp(gst[g, 0:1, cols] - top) / total
+        coef[G:G + 1, cols] = dotted / total
+
+    brim = jnp.where(2 * z < NZ, 0, NZ - 1)
+    core_z = jnp.where(2 * z < NZ, 1, NZ - 2)
+
+    def grads(n, zb):
+        cols = m128(zb, ZB)
+        coefs(zb)
+        dqt[...] = jnp.zeros_like(dqt)
+
+        @pl.loop(0, NC)
+        def _(c):
+            w, off = coef[pl.ds(c, 1), cols], coef[G:G + 1, cols]
+            part_q = None
+            for i in range(CH // FR):
+                at, tok = pl.ds(i * FR, FR), m128(c * (CH // FR) + i, FR)
+                p = ebuf[tok, cols] * w
+                t = (p * (dpb[tok, cols] - off)).astype(BF16)
+                dv = dot(p.astype(BF16), gb[cols, :])
+                dk = dot(t, qb[cols, :])
+                dq = dot(ktb[:, tok], t)
+                part_q = dq if part_q is None else part_q + dq
+                if n:
+                    dk += tmp[c, at, 0:D]
+                    dv += tmp[c, at, D:2 * D]
+                if n < NZ - 1:
+                    tmp[c, at, 0:D] = dk
+                    tmp[c, at, D:2 * D] = dv
+                else:
+                    kv[0, tok, 0:D] = (scale * dk).astype(BF16)
+                    kv[0, tok, D:2 * D] = dv.astype(BF16)
+            dqt[...] += part_q
+            if n == NZ - 1:
+                kv_copy(c, near(1)[1]).start()
         for i in range(ZB // D):
-            t = (scale * dqt[:, pl.ds(zb * ZB + i * D, D)].T).astype(BF16)
+            t = (scale * dqt[:, pl.ds(i * D, D)].T).astype(BF16)
             for k in range(D // RZ):
                 m = i * (D // RZ) + k
-                dqs[pl.ds(zb * RZ, RZ), pl.ds(m * D, D)] = t[k * RZ:(k + 1) * RZ, :]
+                dqs[m128(zb, RZ), pl.ds(m * D, D)] = t[k * RZ:(k + 1) * RZ, :]
+
+        @pl.when(zb != z)
+        def _():
+            d_copy(zb, z).start()
+
+    for f in range(NK // FR):
+        ktb[:, pl.ds(f * FR, FR)] = kb[pl.ds(f * FR, FR), :].astype(F32).T.astype(BF16)
+    grads(0, NZ - 1 - core_z)
+    landed(NZ - 3)
+    grads(1, core_z)
+    grads(2, NZ - 1 - brim)
+    landed(NZ - 2)
+    grads(3, brim)
     HW = JW // 2
 
     def half(u):
         return pl.ds(u * HW, HW)
 
-    def d_copy(u, z_to, z_from, peer):
-        return remote(dqs.at[m128(z_to, RZ), half(u)], dqin.at[z_from, :, half(u)], ds.at[u, z_to], dr.at[u, z_from], peer)
-
-    def a_copy(u, z_to, z_from, peer):
+    def a_copy(kind, u, z_to, z_from):
         here = dqall.at[j, m128(z_from, RZ), half(u)]
-        return remote(here, here, as_.at[u, z_to], ar.at[u, z_from], peer)
+        return remote(here, here, as_.at[kind, u, z_to], ar.at[u, z_from], z_to * G + j)
+
+    def a_own(u, act):
+        @pl.when(inner)
+        def _():
+            for d in range(1, NZ):
+                act(a_copy(0, u, far(d)[0], z))
+
+        @pl.when(jnp.logical_not(inner))
+        def _():
+            act(a_copy(0, u, jnp.where(low, NZ - 2, 1), z))
+
+    def a_onward(u, act):
+        act(a_copy(1, u, NZ - 1 - z, brim))
+        act(a_copy(1, u, NZ - 1 - brim, brim))
 
     def y_copy(u, d, j_from, peer, kind):
         here = dqall.at[j_from, :, half(u)]
         return remote(here, here, ys.at[kind, u], yr.at[kind, u], peer)
 
-    for u in range(2):
-        for d in range(1, NZ):
-            send(d_copy(u, far(d)[0], z, far(d)[2]))
+    landed(NZ - 1)
     for c in local_x:
         c.wait()
 
-    def c_copy(side, b, h, peer):
-        return remote(part.at[h, b], rin.at[side, b, h], cs.at[b, h], cr.at[side, b, h], peer)
-
-    def weigh(b, h, slot):
+    def c_copy(side, b, h, i, peer):
+        at = m128(i, FB)
+        return remote(part.at[h, b, at], rin.at[side, b, h, at], cs.at[b, h, i], cr.at[side, b, h, i], peer)
+
+    def weigh(s, h):
         for i in range(2):
-            tmp[slot, pl.ds(i * FB, FB), :] = dot(vis[b, :, i * FB:(i + 1) * FB], kv[h], TN)
+            tmp[h * NZ + s, pl.ds(i * FB, FB), :] = dot(vis[band(s), :, i * FB:(i + 1) * FB], kv[h], TN)
 
     def gather(s):
         b = band(s)
+        x_copy(1, b, x, near(2)[0], me).wait_recv()
+        send(f_copy(1, b, True))
         pass_copy(b, near(3)[0], me).wait_recv()
         send(f_copy(2, b, True))
         for kind in range(3):
             f_copy(kind, b, False).wait_recv()
 
-    def onward(s, h, between=None):
+    def hop(s):
         b = band(s)
-        weigh(b, h, 0)
         side = (b < z).astype(jnp.int32)
-        fed = jnp.where(b > z, z > 0, z < NZ - 1)
-        out = c_copy(side, b, h, (z + 1 - 2 * side) * G + j)
-
-        def pass_on(extra):
-            part[h, b] = (tmp[0] + extra if extra is not None else tmp[0]).astype(BF16)
-            out.start()
+        return b, side, jnp.where(b > z, low, high), (z + 1 - 2 * side) * G + j
+
+    def first(s, h):
+        weigh(s, h)
+        b, side, fed, peer = hop(s)
 
         @pl.when(jnp.logical_not(fed))
         def _():
-            pass_on(None)
-        if between is not None:
-            between()
+            for i in (1 - y, y):
+                at = m128(i, FB)
+                part[h, b, at] = tmp[h * NZ + s, at].astype(BF16)
+                c_copy(side, b, h, i, peer).start()
+
+    def later(s, h):
+        b, side, fed, peer = hop(s)
 
         @pl.when(fed)
         def _():
-            c_copy(side, b, h, me).wait_recv()
-            pass_on(rin[side, b, h].astype(F32))
-        sends.append(out)
+            for i in (1 - y, y):
+                at = m128(i, FB)
+                c_copy(side, b, h, i, me).wait_recv()
+                part[h, b, at] = (tmp[h * NZ + s, at] + rin[side, b, h, at].astype(F32)).astype(BF16)
+                c_copy(side, b, h, i, peer).start()
 
     def e_copy(h, peer):
         return remote(ybs.at[h], ybr.at[h], es.at[h], er.at[h], peer)
 
+    outs = []
+
+    def settle(head, slot, grad):
+        cols = m128(head, D)
+        for a, out in enumerate((kw_out, vw_out)):
+            wres[a, :, cols] = grad[:, a * D:(a + 1) * D]
+            c = pltpu.make_async_copy(wres.at[a, :, cols], out.at[:, cols], ws.at[a, slot])
+            c.start()
+            outs.append(c)
+
     def finish(h):
-        @pl.when(z > 0)
+        own = h * NZ + NZ - 1
+        for i in (1 - y, y):
+            at = m128(i, FB)
+            for side, there in ((0, low), (1, high)):
+                @pl.when(there)
+                def _():
+                    c_copy(side, z, h, i, me).wait_recv()
+                    tmp[own, at] += rin[side, z, h, at].astype(F32)
+            if i is y:
+                settle(j ^ h, h, tmp[own, at])
+            else:
+                ybs[h] = tmp[own, at].astype(BF16)
+                send(e_copy(h, near(2)[1]))
+
+    def summed_dq():
+        mine = dqs[m128(z, RZ), :].astype(F32)
+        for d in range(1, NZ):
+            d_copy(z, far(d)[1]).wait_recv()
+            mine += dqin[far(d)[1]].astype(F32)
+        dqall[j, m128(z, RZ), :] = mine.astype(BF16)
+        for u in range(2):
+            a_own(u, lambda c: c.start())
+
+    def relay_dq(u):
+        @pl.when(inner)
         def _():
-            c_copy(0, z, h, me).wait_recv()
-            tmp[1 + h] += rin[0, z, h].astype(F32)
-
-        @pl.when(z < NZ - 1)
-        def _():
-            c_copy(1, z, h, me).wait_recv()
-            tmp[1 + h] += rin[1, z, h].astype(F32)
-        ybs[h] = tmp[1 + h, m128(1 - y, FB), :].astype(BF16)
-        send(e_copy(h, near(2)[1]))
-        at = m128(j ^ h, D)
-        kw_out[:, at] = tmp[1 + h, m128(y, FB), 0:D]
-        vw_out[:, at] = tmp[1 + h, m128(y, FB), D:2 * D]
-
-    def summed_dq(u):
-        mine = dqs[m128(z, RZ), half(u)].astype(F32)
-        for d in range(1, NZ):
-            d_copy(u, z, far(d)[1], me).wait_recv()
-            mine += dqin[far(d)[1], :, half(u)].astype(F32)
-        dqall[j, m128(z, RZ), half(u)] = mine.astype(BF16)
-        for d in range(1, NZ):
-            send(a_copy(u, far(d)[0], z, far(d)[2]))
+            a_copy(0, u, z, brim).wait_recv()
+            a_onward(u, lambda c: c.start())
 
     def shared_dq(u):
         for d in range(1, NZ):
-            a_copy(u, z, far(d)[1], me).wait_recv()
+            b = far(d)[1]
+
+            @pl.when(jnp.logical_not(inner) | (b != brim))
+            def _():
+                a_copy(0, u, z, b).wait_recv()
         send(y_copy(u, 1, j, near(1)[1], 0))
         send(y_copy(u, 2, j, near(2)[1], 1))
 
     gather(0)
-    onward(0, 0, lambda: summed_dq(0))
+    first(0, 0)
+    summed_dq()
     gather(1)
-    onward(1, 0, lambda: summed_dq(1))
+    first(1, 0)
+    later(0, 0)
+    relay_dq(0)
+    relay_dq(1)
     gather(2)
-    onward(2, 0)
+    first(2, 0)
+    later(1, 0)
     gather(3)
-    weigh(z, 0, 1)
     for c in range(NC):
         kv_copy(c, me).wait_recv()
-    onward(0, 1, lambda: shared_dq(0))
-    onward(1, 1, lambda: shared_dq(1))
-    onward(2, 1)
-    weigh(z, 1, 2)
-    finish(0)
+    first(0, 1)
+    shared_dq(0)
+    shared_dq(1)
+    for s in range(1, NZ - 1):
+        first(s, 1)
+    later(2, 0)
+    weigh(3, 0)
+    weigh(3, 1)
     y_copy(0, 1, near(1)[0], me, 0).wait_recv()
     send(y_copy(0, 2, near(1)[0], near(2)[1], 2))
+    later(0, 1)
     y_copy(1, 2, near(2)[0], me, 1).wait_recv()
     send(y_copy(1, 1, near(2)[0], near(1)[1], 2))
-    finish(1)
-
-    outs = []
+    later(1, 1)
+    later(2, 1)
+    finish(0)
 
     def put(i):
         c = pltpu.make_async_copy(dqall.at[j ^ i], q_out.at[:, m128(j ^ i, JW)], loc.at[i])
@@ -809,15 +907,62 @@
     y_copy(0, 2, near(3)[0], me, 2).wait_recv()
     y_copy(1, 1, near(3)[0], me, 2).wait_recv()
     put(3)
+    finish(1)
     for h in range(2):
         e_copy(h, me).wait_recv()
-        at = m128(j ^ (2 + h), D)
-        kw_out[:, at] = ybr[h, :, 0:D].astype(F32)
-        vw_out[:, at] = ybr[h, :, D:2 * D].astype(F32)
+        settle(j ^ (2 + h), 2 + h, ybr[h].astype(F32))
     for c in outs:
         c.wait()
     for c in sends:
         c.wait_send()
+    for k in range(NZ):
+        zq_each(lambda c: c.wait_send(), band(NZ - 1 - k), False)
+    for u in range(2):
+        a_own(u, lambda c: c.wait_send())
+        pl.when(inner)(lambda: a_onward(u, lambda c: c.wait_send()))
+    for s in range(NZ - 1):
+        b, side, fed, peer = hop(s)
+        for h in range(2):
+            for i in range(2):
+                c_copy(side, b, h, i, peer).wait_send()
+    for d in range(1, NZ):
+        d_copy(far(d)[0], z).wait_send()
+    for c in range(NC):
+        kv_copy(c, near(1)[1]).wait_send()
+
+
+def deliver_kernel(parts, *refs):
+    n = len(parts)
+    srcs, dsts, bufs, ins, outs = refs[:n], refs[n:2 * n], refs[2 * n:3 * n], refs[3 * n], refs[3 * n + 1]
+    moves, k = [], 0
+    for src, dst, buf, p in zip(srcs, dsts, bufs, parts):
+        step = src.shape[0] // p
+        for i in range(p):
+            at = pl.ds(i * step, step)
+            moves.append((pltpu.make_async_copy(src.at[at], buf.at[at], ins.at[k]),
+                          pltpu.make_async_copy(buf.at[at], dst.at[at], outs.at[k])))
+            k += 1
+    for a, _ in moves:
+        a.start()
+    for a, b in moves:
+        a.wait()
+        b.start()
+    for _, b in moves:
+        b.wait()
+
+
+def deliver(*arrays):
+    parts = [4, 1, 1]
+    anyspec = pl.BlockSpec(memory_space=pl.ANY)
+    return pl.pallas_call(
+        functools.partial(deliver_kernel, parts),
+        out_shape=[jax.ShapeDtypeStruct(a.shape, a.dtype) for a in arrays],
+        in_specs=[anyspec] * len(arrays),
+        out_specs=[anyspec] * len(arrays),
+        scratch_shapes=[pltpu.VMEM(a.shape, a.dtype) for a in arrays]
+        + [pltpu.SemaphoreType.DMA((sum(parts),)), pltpu.SemaphoreType.DMA((sum(parts),))],
+        compiler_params=pltpu.CompilerParams(vmem_limit_bytes=67043328),
+    )(*arrays)
 
 
 def plane_shards(T, text_queries, text_grads, vision_keys, video_value_rows, vision, lengths, frame_range):
@@ -839,10 +984,10 @@
     D = pltpu.SemaphoreType.DMA
     W2 = 2 * HEAD_WIDTH
     pairs = []
-    for a, b in (((2, G),) * 2, ((2, NZ),) * 2, ((2, G),) * 2, ((3, NZ),) * 2, ((3, NZ),) * 2, ((NZ, NZ),) * 2, ((cfg["NC"],),) * 2,
-                 ((2, NZ),) * 2, ((2, NZ),) * 2, ((3, 2),) * 2, ((NZ, 2), (2, NZ, 2)), ((2,),) * 2):
+    for a, b in (((2, G),) * 2, ((2, 2, NZ), (2, NZ)), ((2, G),) * 2, ((3, NZ),) * 2, ((3, NZ),) * 2, ((NZ, NZ),) * 2, ((cfg["NC"],),) * 2,
+                 ((NZ,),) * 2, ((2, 2, NZ), (2, NZ)), ((3, 2),) * 2, ((NZ, 2, 2), (2, NZ, 2, 2)), ((2,),) * 2):
         pairs += [D(a), D(b)]
-    return pl.pallas_call(
+    q_grad, kw, vw = pl.pallas_call(
         functools.partial(plane_kernel, cfg),
         out_shape=(
             jax.ShapeDtypeStruct((T * R, QW), BF16),
@@ -850,7 +995,7 @@
             jax.ShapeDtypeStruct((FB, kv_width), F32),
         ),
         in_specs=[anyspec] * 5 + [sm] * 2,
-        out_specs=(anyspec, vm, vm),
+        out_specs=(anyspec,) * 3,
         scratch_shapes=[
             V((T * R, JW), BF16), V((T * R, JW), BF16),
             V((NR, HEAD_WIDTH), BF16), V((NR, HEAD_WIDTH), BF16),
@@ -859,10 +1004,11 @@
             V((NK, NR), F32), V((NK, NR), F32),
             V((8, NR), F32), V((NZ, 8, NR), F32), V((8, NR), F32), V((8, NR), jnp.int32),
             V((2, NK, W2), BF16),
-            V((HEAD_WIDTH, NR), F32), V((T * R, JW), BF16),
+            V((HEAD_WIDTH, M * RZ), F32), V((T * R, JW), BF16),
             V((NZ, RZ, JW), BF16), V((G, T * R, JW), BF16),
-            V((G, 8, NR), F32),
-            V((3, 2 * FB, W2), F32), V((2, NZ, 2 * FB, W2), BF16), V((2, NZ, 2, 2 * FB, W2), BF16),
+            V((G, 8, NR), F32), V((HEAD_WIDTH, NK), BF16),
+            V((2, FB, kv_width), F32), D((2, 4)),
+            V((2 * NZ, 2 * FB, W2), F32), V((2, NZ, 2 * FB, W2), BF16), V((2, NZ, 2, 2 * FB, W2), BF16),
             V((2, FB, W2), BF16), V((2, FB, W2), BF16),
             D((4,)), D((NZ, 2)),
         ] + pairs,
@@ -870,6 +1016,7 @@
             collective_id=0, has_side_effects=True, vmem_limit_bytes=67043328
         ),
     )(text_queries, text_grads, vision_keys, video_value_rows, vision, lengths, frame_range.T)
+    return deliver(q_grad, kw, vw)
 
 
 def solution(mesh):

time: 123 us -> 102 us (0.83)
  Pallas kernels: 118 us -> 101 us
  local copies, waits for them, and re-layouts: 4.81 us -> 0 us
    pallas_call x1, Pallas kernels: 118 us -> 98.2 us  [plane_shards(): pl.pallas_call(functools.partial(plane_kernel, cfg), out_shape=(jax.Shape...]
    unnamed x7 -> x0, local copies, waits for them, and re-layouts: 4.81 us -> none
    pallas_call x0 -> x1, Pallas kernels: none -> 2.8 us  [deliver(): pl.pallas_call(functools.partial(deliver_kernel, parts), out_shape=[jax.S...]
where the time goes in v2:
time: 102 us
  Pallas kernels  101 us (99%)
    pallas_call x1, Pallas kernels, plane_shards(): pl.pallas_call(functools.partial(plane_kernel, cfg), out_shape=(jax.Shape...  98.2 us
    pallas_call x1, Pallas kernels, deliver(): pl.pallas_call(functools.partial(deliver_kernel, parts), out_shape=[jax.S...  2.8 us

profile of v2, /device:TPU:0, one launch (start us, length us, event | category | flops | bytes accessed | tf_op | source)
XLA Modules:
  0.0 101.8 jit_solution(4769274511415251335)
XLA Ops:
  0.6 98.2 %shard_map.94 = (bf16[256,4096]{1,0:T(8,128)(2,1)}, f32[256,512]{1,0:T(8,128)}, f32[256,512]{1,0:T(8,128)}) custom-call(bf16[16,4096]{1,0:T(8,128)(2,1)} %q_in.1, bf16[16,4096]{1,0:T(8,128)(2,1)} %g_in.1, bf16[512,512]{1,0:T(8,128)(2,1)} %k_in.1, bf16[512,512]{1,0:T(8,128)(2,1)} %v_in.1, bf16[512,4096]{1,0:T(8,128)(2,1)} %x_in.1, s32[8]{0:T(128)} %lens.1, ...), custom_call_target="tpu_custom_call" | custom-call | tf_op jit(solution)/shard_map/pallas_call | solution.py:990
  98.9 2.8 %shard_map.95 = (bf16[256,4096]{1,0:T(8,128)(2,1)}, f32[256,512]{1,0:T(8,128)}, f32[256,512]{1,0:T(8,128)}) custom-call(bf16[256,4096]{1,0:T(8,128)(2,1)} %get-tuple-element.6.refs_0_, f32[256,512]{1,0:T(8,128)} %get-tuple-element.7.refs_1_, f32[256,512]{1,0:T(8,128)} %get-tuple-element.8.refs_2_), custom_call_target="tpu_custom_call" | custom-call | tf_op jit(solution)/shard_map/pallas_call | solution.py:957

commit v3 on v2

--- a/solution.py
+++ b/solution.py
@@ -403,9 +403,9 @@
     return q_grad, kw, vw
 
 
-def plane_kernel(cfg, q_in, g_in, k_in, v_in, x_in, lens, frames, q_out, kw_out, vw_out,
+def plane_kernel(cfg, q_in, g_in, k_in, v_in, x_in, lens_in, frames_in, q_out, kw_out, vw_out,
                  qraw, graw, qb, gb, kb, vb, vis, ebuf, dpb, stat, stin, coef, lim, kv, dqt, dqs, dqin, dqall,
-                 gst, ktb, wres, ws, tmp, part, rin, ybs, ybr, loc, lx, qs, qr, zs, zr, ks, kr, xs, xr, fs, fr, ss, sr, kvs, kvr,
+                 gst, ktb, wres, ws, lens, frames, tmp, part, rin, ybs, ybr, loc, lx, qs, qr, zs, zr, ks, kr, xs, xr, fs, fr, ss, sr, kvs, kvr,
                  ds, dr, as_, ar, ys, yr, cs, cr, es, er):
     G, NZ, M, R, FR, NC = cfg["G"], cfg["NZ"], cfg["M"], cfg["R"], cfg["FR"], cfg["NC"]
     rows, NK, NR, JW, FB, RZ = cfg["rows"], cfg["NK"], cfg["NR"], cfg["JW"], cfg["FB"], cfg["RZ"]
@@ -470,8 +470,8 @@
         here = (qraw, graw)[a].at[m128(b, RZ)]
         return remote(here, here, zs.at[side, a, b], zr.at[a, b], (z + 1 - 2 * side) * G + j)
 
-    def zq_each(act, b, into):
-        for a in range(2):
+    def zq_each(act, b, into, which=(0, 1)):
+        for a in which:
             if into:
                 zq_copy(0, a, b).wait_recv()
 
@@ -510,6 +510,8 @@
         pltpu.make_async_copy(g_in.at[:, m128(j, JW)], graw.at[own_rows(me)], loc.at[1]),
         pltpu.make_async_copy(k_in.at[:, m128(j, D)], kb.at[m128(j, rows)], loc.at[2]),
         pltpu.make_async_copy(v_in.at[:, m128(j, D)], vb.at[m128(j, rows)], loc.at[3]),
+        pltpu.make_async_copy(lens_in, lens, loc.at[4]),
+        pltpu.make_async_copy(frames_in, frames, loc.at[5]),
     ]
     for c in local:
         c.start()
@@ -525,6 +527,8 @@
             local_x.append(pltpu.make_async_copy(
                 x_in.at[:, m128(b * G + 2 * h + x, FB)], vis.at[b, m128(j, rows), pl.ds(h * FB, FB)], lx.at[b, h]))
 
+    for c in local[4:]:
+        c.wait()
     col = lax.broadcasted_iota(jnp.int32, (1, NR), 1)
     text = (col // ZB) * RZ + col % RZ
     seg = jnp.zeros((1, NR), jnp.int32)
@@ -553,35 +557,38 @@
             send(x_copy(1, band(s), x, j, near(2)[1]))
     for c in local_x:
         c.start()
-    for c in local[2:]:
+    for c in local[2:4]:
         c.wait()
 
     n_frames = rows // FR
 
-    def totals(g, zb):
+    def tokens(g, f):
+        return m128(g * n_frames + f, FR)
+
+    def scored(g, zb):
         cols = m128(zb, ZB)
         lo, hi = lim[0:1, cols], lim[1:2, cols]
         base = z * G * n_frames + g * n_frames
-
-        def tokens(f):
-            return m128(g * n_frames + f, FR)
-
         top = jnp.full((1, ZB), NEG_FILL, F32)
         for f in range(n_frames):
             ok = (lo <= base + f) & (base + f < hi)
-            sc = jnp.where(ok, dot(kb[tokens(f), :], qb[cols, :], NT) * scale, NEG_FILL)
-            ebuf[tokens(f), cols] = sc
+            sc = jnp.where(ok, dot(kb[tokens(g, f), :], qb[cols, :], NT) * scale, NEG_FILL)
+            ebuf[tokens(g, f), cols] = sc
             top = jnp.maximum(top, jnp.max(sc, axis=0, keepdims=True))
+        gst[g, 0:1, cols] = top
+
+    def summed(g, zb):
+        cols = m128(zb, ZB)
+        top = gst[g, 0:1, cols]
         total = jnp.zeros((1, ZB), F32)
         dotted = jnp.zeros((1, ZB), F32)
         for f in range(n_frames):
-            dp = dot(vb[tokens(f), :], gb[cols, :], NT)
-            e = jnp.exp(ebuf[tokens(f), cols] - top)
-            ebuf[tokens(f), cols] = e
-            dpb[tokens(f), cols] = dp
+            dp = dot(vb[tokens(g, f), :], gb[cols, :], NT)
+            e = jnp.exp(ebuf[tokens(g, f), cols] - top)
+            ebuf[tokens(g, f), cols] = e
+            dpb[tokens(g, f), cols] = dp
             total += jnp.sum(e, axis=0, keepdims=True)
             dotted += jnp.sum(e * dp, axis=0, keepdims=True)
-        gst[g, 0:1, cols] = top
         gst[g, 1:2, cols] = total
         gst[g, 2:3, cols] = dotted
 
@@ -604,7 +611,7 @@
         stat[1:2, cols] = total
         stat[2:3, cols] = dotted
         for d in range(1, NZ):
-            send(s_copy(zb, far(d)[0], z, far(d)[2]))
+            s_copy(zb, far(d)[0], z, far(d)[2]).start()
 
     def landed(s):
         b = band(s)
@@ -616,8 +623,14 @@
 
     have_g, have_z = {0}, set()
 
-    def arrive(k):
-        zq_each(lambda c: c.start(), band(NZ - 1 - k), True)
+    def arrive(k, which=(0, 1)):
+        zq_each(lambda c: c.start(), band(NZ - 1 - k), True, which)
+
+    def head_rows(zb, which=(0, 1)):
+        for a in which:
+            raw, buf = (qraw, graw)[a], (qb, gb)[a]
+            for m in range(M):
+                buf[m128(zb * M + m, RZ), :] = raw[m128(zb, RZ), m * D:(m + 1) * D]
 
     def block(d, k):
         zb = band(NZ - 1 - k)
@@ -629,10 +642,19 @@
             have_z.add(k)
             if k:
                 pl.when(jnp.logical_not(inner))(lambda: arrive(k))
-            for raw, buf in ((qraw, qb), (graw, gb)):
-                for m in range(M):
-                    buf[m128(zb * M + m, RZ), :] = raw[m128(zb, RZ), m * D:(m + 1) * D]
-        totals(j ^ d, zb)
+            head_rows(zb)
+        scored(j ^ d, zb)
+        summed(j ^ d, zb)
+
+    def last_block(k, waits):
+        zb = band(NZ - 1 - k)
+        for a, work in ((0, scored), (1, summed)):
+            if waits:
+                arrive(k, (a,))
+            head_rows(zb, (a,))
+            for d in range(G):
+                work(j ^ d, zb)
+        plane_totals(zb)
 
     block(0, 0)
     block(1, 0)
@@ -651,12 +673,12 @@
     plane_totals(band(NZ - 1))
     block(3, 1)
     plane_totals(band(NZ - 2))
-    for k in range(2, NZ):
-        for d in range(G):
-            block(d, k)
-        plane_totals(band(NZ - 1 - k))
-        if k < NZ - 1:
-            landed(k - 2)
+    for d in range(G):
+        block(d, 2)
+    plane_totals(band(NZ - 3))
+    landed(0)
+    pl.when(inner)(lambda: last_block(3, False))
+    pl.when(jnp.logical_not(inner))(lambda: last_block(3, True))
 
     CH = NK // NC
 
@@ -758,11 +780,16 @@
         act(a_copy(1, u, NZ - 1 - z, brim))
         act(a_copy(1, u, NZ - 1 - brim, brim))
 
-    def y_copy(u, d, j_from, peer, kind):
-        here = dqall.at[j_from, :, half(u)]
+    QW = JW // 4
+
+    def y_copy(u, j_from, peer, kind):
+        here = dqall.at[j_from, :, pl.ds(u * QW, QW)]
         return remote(here, here, ys.at[kind, u], yr.at[kind, u], peer)
 
-    landed(NZ - 1)
+    def y_pass(u, frm, to):
+        y_copy(u, near(frm)[0], me, frm - 1).wait_recv()
+        send(y_copy(u, near(frm)[0], near(to)[1], 2))
+
     for c in local_x:
         c.wait()
 
@@ -853,18 +880,21 @@
             a_copy(0, u, z, brim).wait_recv()
             a_onward(u, lambda c: c.start())
 
-    def shared_dq(u):
-        for d in range(1, NZ):
-            b = far(d)[1]
-
-            @pl.when(jnp.logical_not(inner) | (b != brim))
-            def _():
-                a_copy(0, u, z, b).wait_recv()
-        send(y_copy(u, 1, j, near(1)[1], 0))
-        send(y_copy(u, 2, j, near(2)[1], 1))
+    def shared_dq():
+        for u in range(2):
+            for d in range(1, NZ):
+                b = far(d)[1]
+
+                @pl.when(jnp.logical_not(inner) | (b != brim))
+                def _():
+                    a_copy(0, u, z, b).wait_recv()
+        for u in range(4):
+            send(y_copy(u, j, near(1)[1], 0))
+            send(y_copy((u + 1) % 4, j, near(2)[1], 1))
 
     gather(0)
     first(0, 0)
+    landed(NZ - 1)
     summed_dq()
     gather(1)
     first(1, 0)
@@ -873,41 +903,40 @@
     relay_dq(1)
     gather(2)
     first(2, 0)
+    shared_dq()
     later(1, 0)
     gather(3)
     for c in range(NC):
         kv_copy(c, me).wait_recv()
     first(0, 1)
-    shared_dq(0)
-    shared_dq(1)
     for s in range(1, NZ - 1):
         first(s, 1)
     later(2, 0)
     weigh(3, 0)
     weigh(3, 1)
-    y_copy(0, 1, near(1)[0], me, 0).wait_recv()
-    send(y_copy(0, 2, near(1)[0], near(2)[1], 2))
-    later(0, 1)
-    y_copy(1, 2, near(2)[0], me, 1).wait_recv()
-    send(y_copy(1, 1, near(2)[0], near(1)[1], 2))
-    later(1, 1)
-    later(2, 1)
-    finish(0)
-
     def put(i):
         c = pltpu.make_async_copy(dqall.at[j ^ i], q_out.at[:, m128(j ^ i, JW)], loc.at[i])
         c.start()
         outs.append(c)
 
     put(0)
-    y_copy(1, 1, near(1)[0], me, 0).wait_recv()
+    y_pass(0, 1, 2)
+    y_pass(1, 2, 1)
+    later(0, 1)
+    y_pass(2, 2, 1)
+    finish(0)
+    y_pass(3, 2, 1)
+    later(1, 1)
+    later(2, 1)
+    for u in range(1, 4):
+        y_copy(u, near(1)[0], me, 0).wait_recv()
     put(1)
-    y_copy(0, 2, near(2)[0], me, 1).wait_recv()
+    y_copy(0, near(2)[0], me, 1).wait_recv()
     put(2)
-    y_copy(0, 2, near(3)[0], me, 2).wait_recv()
-    y_copy(1, 1, near(3)[0], me, 2).wait_recv()
+    finish(1)
+    for u in range(4):
+        y_copy(u, near(3)[0], me, 2).wait_recv()
     put(3)
-    finish(1)
     for h in range(2):
         e_copy(h, me).wait_recv()
         settle(j ^ (2 + h), 2 + h, ybr[h].astype(F32))
@@ -929,6 +958,9 @@
         d_copy(far(d)[0], z).wait_send()
     for c in range(NC):
         kv_copy(c, near(1)[1]).wait_send()
+    for zb in range(NZ):
+        for d in range(1, NZ):
+            s_copy(zb, far(d)[0], z, far(d)[2]).wait_send()
 
 
 def deliver_kernel(parts, *refs):
@@ -952,7 +984,7 @@
 
 
 def deliver(*arrays):
-    parts = [4, 1, 1]
+    parts = [8, 2, 2]
     anyspec = pl.BlockSpec(memory_space=pl.ANY)
     return pl.pallas_call(
         functools.partial(deliver_kernel, parts),
@@ -979,13 +1011,12 @@
                NS=lengths.shape[0])
     anyspec = pl.BlockSpec(memory_space=pl.ANY)
     vm = pl.BlockSpec(memory_space=pltpu.VMEM)
-    sm = pl.BlockSpec(memory_space=pltpu.SMEM)
     V = pltpu.VMEM
     D = pltpu.SemaphoreType.DMA
     W2 = 2 * HEAD_WIDTH
     pairs = []
     for a, b in (((2, G),) * 2, ((2, 2, NZ), (2, NZ)), ((2, G),) * 2, ((3, NZ),) * 2, ((3, NZ),) * 2, ((NZ, NZ),) * 2, ((cfg["NC"],),) * 2,
-                 ((NZ,),) * 2, ((2, 2, NZ), (2, NZ)), ((3, 2),) * 2, ((NZ, 2, 2), (2, NZ, 2, 2)), ((2,),) * 2):
+                 ((NZ,),) * 2, ((2, 2, NZ), (2, NZ)), ((3, 4),) * 2, ((NZ, 2, 2), (2, NZ, 2, 2)), ((2,),) * 2):
         pairs += [D(a), D(b)]
     q_grad, kw, vw = pl.pallas_call(
         functools.partial(plane_kernel, cfg),
@@ -994,7 +1025,7 @@
             jax.ShapeDtypeStruct((FB, kv_width), F32),
             jax.ShapeDtypeStruct((FB, kv_width), F32),
         ),
-        in_specs=[anyspec] * 5 + [sm] * 2,
+        in_specs=[anyspec] * 7,
         out_specs=(anyspec,) * 3,
         scratch_shapes=[
             V((T * R, JW), BF16), V((T * R, JW), BF16),
@@ -1008,9 +1039,10 @@
             V((NZ, RZ, JW), BF16), V((G, T * R, JW), BF16),
             V((G, 8, NR), F32), V((HEAD_WIDTH, NK), BF16),
             V((2, FB, kv_width), F32), D((2, 4)),
+            pltpu.SMEM(lengths.shape, jnp.int32), pltpu.SMEM(frame_range.shape[::-1], jnp.int32),
             V((2 * NZ, 2 * FB, W2), F32), V((2, NZ, 2 * FB, W2), BF16), V((2, NZ, 2, 2 * FB, W2), BF16),
             V((2, FB, W2), BF16), V((2, FB, W2), BF16),
-            D((4,)), D((NZ, 2)),
+            D((6,)), D((NZ, 2)),
         ] + pairs,
         compiler_params=pltpu.CompilerParams(
             collective_id=0, has_side_effects=True, vmem_limit_bytes=67043328

time: 102 us -> 96.9 us (0.950)
  Pallas kernels: 101 us -> 95.3 us
    pallas_call x1, Pallas kernels: 98.2 us -> 92.5 us  [plane_shards(): pl.pallas_call(functools.partial(plane_kernel, cfg), out_shape=(jax.Shape...]
where the time goes in v3:
time: 96.9 us; the launch traced here: 96.1 us
  Pallas kernels  95.3 us (98%)
    pallas_call x1, Pallas kernels, plane_shards(): pl.pallas_call(functools.partial(plane_kernel, cfg), out_shape=(jax.Shape...  92.5 us
    pallas_call x1, Pallas kernels, deliver(): pl.pallas_call(functools.partial(deliver_kernel, parts), out_shape=[jax.S...  2.81 us

profile of v3, /device:TPU:0, one launch (start us, length us, event | category | flops | bytes accessed | tf_op | source)
XLA Modules:
  0.0 96.1 jit_solution(2022823332674544841)
XLA Ops:
  0.6 92.5 %shard_map.94 = (bf16[256,4096]{1,0:T(8,128)(2,1)}, f32[256,512]{1,0:T(8,128)}, f32[256,512]{1,0:T(8,128)}) custom-call(bf16[16,4096]{1,0:T(8,128)(2,1)} %q_in.1, bf16[16,4096]{1,0:T(8,128)(2,1)} %g_in.1, bf16[512,512]{1,0:T(8,128)(2,1)} %k_in.1, bf16[512,512]{1,0:T(8,128)(2,1)} %v_in.1, bf16[512,4096]{1,0:T(8,128)(2,1)} %x_in.1, s32[8]{0:T(128)} %lens_in.1, ...), custom_call_target="tpu_custom_call" | custom-call | tf_op jit(solution)/shard_map/pallas_call | solution.py:1021
  93.1 2.8 %shard_map.95 = (bf16[256,4096]{1,0:T(8,128)(2,1)}, f32[256,512]{1,0:T(8,128)}, f32[256,512]{1,0:T(8,128)}) custom-call(bf16[256,4096]{1,0:T(8,128)(2,1)} %get-tuple-element.6.refs_0_, f32[256,512]{1,0:T(8,128)} %get-tuple-element.7.refs_1_, f32[256,512]{1,0:T(8,128)} %get-tuple-element.8.refs_2_), custom_call_target="tpu_custom_call" | custom-call | tf_op jit(solution)/shard_map/pallas_call | solution.py:989

commit v4 on v3

--- a/solution.py
+++ b/solution.py
@@ -404,7 +404,7 @@
 
 
 def plane_kernel(cfg, q_in, g_in, k_in, v_in, x_in, lens_in, frames_in, q_out, kw_out, vw_out,
-                 qraw, graw, qb, gb, kb, vb, vis, ebuf, dpb, stat, stin, coef, lim, kv, dqt, dqs, dqin, dqall,
+                 qraw, graw, qb, gb, kb, vb, vis, ebuf, dpb, stat, stin, coef, lim, kv, kvn, dqt, dqs, dqin, dqall,
                  gst, ktb, wres, ws, lens, frames, tmp, part, rin, ybs, ybr, loc, lx, qs, qr, zs, zr, ks, kr, xs, xr, fs, fr, ss, sr, kvs, kvr,
                  ds, dr, as_, ar, ys, yr, cs, cr, es, er):
     G, NZ, M, R, FR, NC = cfg["G"], cfg["NZ"], cfg["M"], cfg["R"], cfg["FR"], cfg["NC"]
@@ -682,9 +682,8 @@
 
     CH = NK // NC
 
-    def kv_copy(c, peer):
-        at = m128(c, CH)
-        return remote(kv.at[0, at], kv.at[1, at], kvs.at[c], kvr.at[c], peer)
+    def kv_copy(p, peer):
+        return remote(kv.at[:, pl.ds(p * D, D)], kvn.at[p], kvs.at[p], kvr.at[p], peer)
 
     def d_copy(z_to, z_from):
         return remote(dqs.at[m128(z_to, RZ)], dqin.at[z_from], ds.at[z_to], dr.at[z_from], z_to * G + j)
@@ -734,11 +733,13 @@
                     tmp[c, at, 0:D] = dk
                     tmp[c, at, D:2 * D] = dv
                 else:
-                    kv[0, tok, 0:D] = (scale * dk).astype(BF16)
-                    kv[0, tok, D:2 * D] = dv.astype(BF16)
+                    kv[tok, 0:D] = (scale * dk).astype(BF16)
+                    kv[tok, D:2 * D] = dv.astype(BF16)
             dqt[...] += part_q
-            if n == NZ - 1:
-                kv_copy(c, near(1)[1]).start()
+
+        if n == NZ - 1:
+            for p in (1, 0):
+                send(kv_copy(p, near(1)[1]))
         for i in range(ZB // D):
             t = (scale * dqt[:, pl.ds(i * D, D)].T).astype(BF16)
             for k in range(D // RZ):
@@ -793,13 +794,18 @@
     for c in local_x:
         c.wait()
 
-    def c_copy(side, b, h, i, peer):
-        at = m128(i, FB)
-        return remote(part.at[h, b, at], rin.at[side, b, h, at], cs.at[b, h, i], cr.at[side, b, h, i], peer)
-
-    def weigh(s, h):
+    def piece(h, p, i):
+        cols = pl.ds(p * D, D) if h else pl.ds(0, 2 * D)
+        return m128(i, FB), cols, (2 + 2 * p + i if h else i)
+
+    def c_copy(side, b, h, p, i, peer):
+        at, cols, n = piece(h, p, i)
+        return remote(part.at[h, b, at, cols], rin.at[side, b, h, at, cols], cs.at[b, n], cr.at[side, b, n], peer)
+
+    def weigh(s, h, p):
         for i in range(2):
-            tmp[h * NZ + s, pl.ds(i * FB, FB), :] = dot(vis[band(s), :, i * FB:(i + 1) * FB], kv[h], TN)
+            at, cols, _ = piece(h, p, i)
+            tmp[h * NZ + s, at, cols] = dot(vis[band(s), :, i * FB:(i + 1) * FB], kvn[p] if h else kv[...], TN)
 
     def gather(s):
         b = band(s)
@@ -815,55 +821,56 @@
         side = (b < z).astype(jnp.int32)
         return b, side, jnp.where(b > z, low, high), (z + 1 - 2 * side) * G + j
 
-    def first(s, h):
-        weigh(s, h)
+    def first(s, h, p=0):
+        weigh(s, h, p)
         b, side, fed, peer = hop(s)
 
         @pl.when(jnp.logical_not(fed))
         def _():
             for i in (1 - y, y):
-                at = m128(i, FB)
-                part[h, b, at] = tmp[h * NZ + s, at].astype(BF16)
-                c_copy(side, b, h, i, peer).start()
-
-    def later(s, h):
+                at, cols, _ = piece(h, p, i)
+                part[h, b, at, cols] = tmp[h * NZ + s, at, cols].astype(BF16)
+                c_copy(side, b, h, p, i, peer).start()
+
+    def later(s, h, p=0):
         b, side, fed, peer = hop(s)
 
         @pl.when(fed)
         def _():
             for i in (1 - y, y):
-                at = m128(i, FB)
-                c_copy(side, b, h, i, me).wait_recv()
-                part[h, b, at] = (tmp[h * NZ + s, at] + rin[side, b, h, at].astype(F32)).astype(BF16)
-                c_copy(side, b, h, i, peer).start()
-
-    def e_copy(h, peer):
-        return remote(ybs.at[h], ybr.at[h], es.at[h], er.at[h], peer)
+                at, cols, _ = piece(h, p, i)
+                c_copy(side, b, h, p, i, me).wait_recv()
+                part[h, b, at, cols] = (tmp[h * NZ + s, at, cols] + rin[side, b, h, at, cols].astype(F32)).astype(BF16)
+                c_copy(side, b, h, p, i, peer).start()
+
+    def e_copy(h, p, peer):
+        cols = piece(h, p, 0)[1]
+        return remote(ybs.at[h, :, cols], ybr.at[h, :, cols], es.at[h + h * p], er.at[h + h * p], peer)
 
     outs = []
 
-    def settle(head, slot, grad):
+    def settle(head, slot, grads_of, grad):
         cols = m128(head, D)
-        for a, out in enumerate((kw_out, vw_out)):
-            wres[a, :, cols] = grad[:, a * D:(a + 1) * D]
-            c = pltpu.make_async_copy(wres.at[a, :, cols], out.at[:, cols], ws.at[a, slot])
+        for n, a in enumerate(grads_of):
+            wres[a, :, cols] = grad[:, n * D:(n + 1) * D]
+            c = pltpu.make_async_copy(wres.at[a, :, cols], (kw_out, vw_out)[a].at[:, cols], ws.at[a, slot])
             c.start()
             outs.append(c)
 
-    def finish(h):
+    def finish(h, p=0):
         own = h * NZ + NZ - 1
         for i in (1 - y, y):
-            at = m128(i, FB)
+            at, cols, _ = piece(h, p, i)
             for side, there in ((0, low), (1, high)):
                 @pl.when(there)
                 def _():
-                    c_copy(side, z, h, i, me).wait_recv()
-                    tmp[own, at] += rin[side, z, h, at].astype(F32)
+                    c_copy(side, z, h, p, i, me).wait_recv()
+                    tmp[own, at, cols] += rin[side, z, h, at, cols].astype(F32)
             if i is y:
-                settle(j ^ h, h, tmp[own, at])
+                settle(j ^ h, h, (p,) if h else (0, 1), tmp[own, at, cols])
             else:
-                ybs[h] = tmp[own, at].astype(BF16)
-                send(e_copy(h, near(2)[1]))
+                ybs[h, :, cols] = tmp[own, at, cols].astype(BF16)
+                send(e_copy(h, p, near(2)[1]))
 
     def summed_dq():
         mine = dqs[m128(z, RZ), :].astype(F32)
@@ -901,19 +908,25 @@
     later(0, 0)
     relay_dq(0)
     relay_dq(1)
+    kv_copy(1, me).wait_recv()
+    first(0, 1, 1)
+    first(1, 1, 1)
+    later(1, 0)
     gather(2)
     first(2, 0)
     shared_dq()
-    later(1, 0)
+    first(2, 1, 1)
+    later(0, 1, 1)
     gather(3)
-    for c in range(NC):
-        kv_copy(c, me).wait_recv()
-    first(0, 1)
-    for s in range(1, NZ - 1):
-        first(s, 1)
+    kv_copy(0, me).wait_recv()
+    for s in range(NZ - 1):
+        first(s, 1, 0)
+    later(1, 1, 1)
     later(2, 0)
-    weigh(3, 0)
-    weigh(3, 1)
+    weigh(3, 0, 0)
+    weigh(3, 1, 1)
+    weigh(3, 1, 0)
+
     def put(i):
         c = pltpu.make_async_copy(dqall.at[j ^ i], q_out.at[:, m128(j ^ i, JW)], loc.at[i])
         c.start()
@@ -922,24 +935,26 @@
     put(0)
     y_pass(0, 1, 2)
     y_pass(1, 2, 1)
-    later(0, 1)
+    later(2, 1, 1)
+    finish(0)
+    later(0, 1, 0)
     y_pass(2, 2, 1)
-    finish(0)
     y_pass(3, 2, 1)
-    later(1, 1)
-    later(2, 1)
+    later(1, 1, 0)
+    later(2, 1, 0)
     for u in range(1, 4):
         y_copy(u, near(1)[0], me, 0).wait_recv()
     put(1)
     y_copy(0, near(2)[0], me, 1).wait_recv()
     put(2)
-    finish(1)
+    finish(1, 1)
+    finish(1, 0)
     for u in range(4):
         y_copy(u, near(3)[0], me, 2).wait_recv()
     put(3)
-    for h in range(2):
-        e_copy(h, me).wait_recv()
-        settle(j ^ (2 + h), 2 + h, ybr[h].astype(F32))
+    for h, p, grads_of in ((0, 0, (0, 1)), (1, 1, (1,)), (1, 0, (0,))):
+        e_copy(h, p, me).wait_recv()
+        settle(j ^ (2 + h), 2 + h, grads_of, ybr[h, :, piece(h, p, 0)[1]].astype(F32))
     for c in outs:
         c.wait()
     for c in sends:
@@ -951,13 +966,11 @@
         pl.when(inner)(lambda: a_onward(u, lambda c: c.wait_send()))
     for s in range(NZ - 1):
         b, side, fed, peer = hop(s)
-        for h in range(2):
+        for h, p in ((0, 0), (1, 0), (1, 1)):
             for i in range(2):
-                c_copy(side, b, h, i, peer).wait_send()
+                c_copy(side, b, h, p, i, peer).wait_send()
     for d in range(1, NZ):
         d_copy(far(d)[0], z).wait_send()
-    for c in range(NC):
-        kv_copy(c, near(1)[1]).wait_send()
     for zb in range(NZ):
         for d in range(1, NZ):
             s_copy(zb, far(d)[0], z, far(d)[2]).wait_send()
@@ -1015,8 +1028,8 @@
     D = pltpu.SemaphoreType.DMA
     W2 = 2 * HEAD_WIDTH
     pairs = []
-    for a, b in (((2, G),) * 2, ((2, 2, NZ), (2, NZ)), ((2, G),) * 2, ((3, NZ),) * 2, ((3, NZ),) * 2, ((NZ, NZ),) * 2, ((cfg["NC"],),) * 2,
-                 ((NZ,),) * 2, ((2, 2, NZ), (2, NZ)), ((3, 4),) * 2, ((NZ, 2, 2), (2, NZ, 2, 2)), ((2,),) * 2):
+    for a, b in (((2, G),) * 2, ((2, 2, NZ), (2, NZ)), ((2, G),) * 2, ((3, NZ),) * 2, ((3, NZ),) * 2, ((NZ, NZ),) * 2, ((2,),) * 2,
+                 ((NZ,),) * 2, ((2, 2, NZ), (2, NZ)), ((3, 4),) * 2, ((NZ, 6), (2, NZ, 6)), ((3,),) * 2):
         pairs += [D(a), D(b)]
     q_grad, kw, vw = pl.pallas_call(
         functools.partial(plane_kernel, cfg),
@@ -1034,7 +1047,7 @@
             V((NZ, NK, 2 * FB), BF16),
             V((NK, NR), F32), V((NK, NR), F32),
             V((8, NR), F32), V((NZ, 8, NR), F32), V((8, NR), F32), V((8, NR), jnp.int32),
-            V((2, NK, W2), BF16),
+            V((NK, W2), BF16), V((2, NK, HEAD_WIDTH), BF16),
             V((HEAD_WIDTH, M * RZ), F32), V((T * R, JW), BF16),
             V((NZ, RZ, JW), BF16), V((G, T * R, JW), BF16),
             V((G, 8, NR), F32), V((HEAD_WIDTH, NK), BF16),

time: 96.9 us -> 95.7 us (0.988)
  no operation moved by 1% of the time
where the time goes in v4:
time: 95.7 us; the launch traced here: 95.5 us
  Pallas kernels  94.7 us (99%)
    pallas_call x1, Pallas kernels, plane_shards(): pl.pallas_call(functools.partial(plane_kernel, cfg), out_shape=(jax.Shape...  91.9 us
    pallas_call x1, Pallas kernels, deliver(): pl.pallas_call(functools.partial(deliver_kernel, parts), out_shape=[jax.S...  2.81 us

profile of v4, /device:TPU:0, one launch (start us, length us, event | category | flops | bytes accessed | tf_op | source)
XLA Modules:
  0.0 95.5 jit_solution(4559260436650562067)
XLA Ops:
  0.6 91.9 %shard_map.94 = (bf16[256,4096]{1,0:T(8,128)(2,1)}, f32[256,512]{1,0:T(8,128)}, f32[256,512]{1,0:T(8,128)}) custom-call(bf16[16,4096]{1,0:T(8,128)(2,1)} %q_in.1, bf16[16,4096]{1,0:T(8,128)(2,1)} %g_in.1, bf16[512,512]{1,0:T(8,128)(2,1)} %k_in.1, bf16[512,512]{1,0:T(8,128)(2,1)} %v_in.1, bf16[512,4096]{1,0:T(8,128)(2,1)} %x_in.1, s32[8]{0:T(128)} %lens_in.1, ...), custom_call_target="tpu_custom_call" | custom-call | tf_op jit(solution)/shard_map/pallas_call | solution.py:1034
  92.6 2.8 %shard_map.95 = (bf16[256,4096]{1,0:T(8,128)(2,1)}, f32[256,512]{1,0:T(8,128)}, f32[256,512]{1,0:T(8,128)}) custom-call(bf16[256,4096]{1,0:T(8,128)(2,1)} %get-tuple-element.6.refs_0_, f32[256,512]{1,0:T(8,128)} %get-tuple-element.7.refs_1_, f32[256,512]{1,0:T(8,128)} %get-tuple-element.8.refs_2_), custom_call_target="tpu_custom_call" | custom-call | tf_op jit(solution)/shard_map/pallas_call | solution.py:1002

commit v5 on v4

--- a/solution.py
+++ b/solution.py
@@ -404,8 +404,8 @@
 
 
 def plane_kernel(cfg, q_in, g_in, k_in, v_in, x_in, lens_in, frames_in, q_out, kw_out, vw_out,
-                 qraw, graw, qb, gb, kb, vb, vis, ebuf, dpb, stat, stin, coef, lim, kv, kvn, dqt, dqs, dqin, dqall,
-                 gst, ktb, wres, ws, lens, frames, tmp, part, rin, ybs, ybr, loc, lx, qs, qr, zs, zr, ks, kr, xs, xr, fs, fr, ss, sr, kvs, kvr,
+                 qraw, graw, qb, gb, kb, vb, vis, ebuf, dpb, stat, stin, coef, lim, kv, kvn, dqt, dqs, dqin,
+                 gst, ktb, lens, frames, tmp, part, rin, ybs, ybr, loc, lx, qs, qr, zs, zr, ks, kr, xs, xr, fs, fr, ss, sr, kvs, kvr,
                  ds, dr, as_, ar, ys, yr, cs, cr, es, er):
     G, NZ, M, R, FR, NC = cfg["G"], cfg["NZ"], cfg["M"], cfg["R"], cfg["FR"], cfg["NC"]
     rows, NK, NR, JW, FB, RZ = cfg["rows"], cfg["NK"], cfg["NR"], cfg["JW"], cfg["FB"], cfg["RZ"]
@@ -760,11 +760,14 @@
     grads(3, brim)
     HW = JW // 2
 
+    def jcols(head, off, n):
+        return pl.ds(pl.multiple_of(head * JW + off, n), n)
+
     def half(u):
         return pl.ds(u * HW, HW)
 
     def a_copy(kind, u, z_to, z_from):
-        here = dqall.at[j, m128(z_from, RZ), half(u)]
+        here = q_out.at[m128(z_from, RZ), jcols(j, u * HW, HW)]
         return remote(here, here, as_.at[kind, u, z_to], ar.at[u, z_from], z_to * G + j)
 
     def a_own(u, act):
@@ -784,7 +787,7 @@
     QW = JW // 4
 
     def y_copy(u, j_from, peer, kind):
-        here = dqall.at[j_from, :, pl.ds(u * QW, QW)]
+        here = q_out.at[:, jcols(j_from, u * QW, QW)]
         return remote(here, here, ys.at[kind, u], yr.at[kind, u], peer)
 
     def y_pass(u, frm, to):
@@ -847,15 +850,10 @@
         cols = piece(h, p, 0)[1]
         return remote(ybs.at[h, :, cols], ybr.at[h, :, cols], es.at[h + h * p], er.at[h + h * p], peer)
 
-    outs = []
-
-    def settle(head, slot, grads_of, grad):
+    def settle(head, grads_of, grad):
         cols = m128(head, D)
         for n, a in enumerate(grads_of):
-            wres[a, :, cols] = grad[:, n * D:(n + 1) * D]
-            c = pltpu.make_async_copy(wres.at[a, :, cols], (kw_out, vw_out)[a].at[:, cols], ws.at[a, slot])
-            c.start()
-            outs.append(c)
+            (kw_out, vw_out)[a][:, cols] = grad[:, n * D:(n + 1) * D]
 
     def finish(h, p=0):
         own = h * NZ + NZ - 1
@@ -867,7 +865,7 @@
                     c_copy(side, z, h, p, i, me).wait_recv()
                     tmp[own, at, cols] += rin[side, z, h, at, cols].astype(F32)
             if i is y:
-                settle(j ^ h, h, (p,) if h else (0, 1), tmp[own, at, cols])
+                settle(j ^ h, (p,) if h else (0, 1), tmp[own, at, cols])
             else:
                 ybs[h, :, cols] = tmp[own, at, cols].astype(BF16)
                 send(e_copy(h, p, near(2)[1]))
@@ -877,7 +875,7 @@
         for d in range(1, NZ):
             d_copy(z, far(d)[1]).wait_recv()
             mine += dqin[far(d)[1]].astype(F32)
-        dqall[j, m128(z, RZ), :] = mine.astype(BF16)
+        q_out[m128(z, RZ), m128(j, JW)] = mine.astype(BF16)
         for u in range(2):
             a_own(u, lambda c: c.start())
 
@@ -927,12 +925,6 @@
     weigh(3, 1, 1)
     weigh(3, 1, 0)
 
-    def put(i):
-        c = pltpu.make_async_copy(dqall.at[j ^ i], q_out.at[:, m128(j ^ i, JW)], loc.at[i])
-        c.start()
-        outs.append(c)
-
-    put(0)
     y_pass(0, 1, 2)
     y_pass(1, 2, 1)
     later(2, 1, 1)
@@ -944,19 +936,14 @@
     later(2, 1, 0)
     for u in range(1, 4):
         y_copy(u, near(1)[0], me, 0).wait_recv()
-    put(1)
     y_copy(0, near(2)[0], me, 1).wait_recv()
-    put(2)
     finish(1, 1)
     finish(1, 0)
     for u in range(4):
         y_copy(u, near(3)[0], me, 2).wait_recv()
-    put(3)
     for h, p, grads_of in ((0, 0, (0, 1)), (1, 1, (1,)), (1, 0, (0,))):
         e_copy(h, p, me).wait_recv()
-        settle(j ^ (2 + h), 2 + h, grads_of, ybr[h, :, piece(h, p, 0)[1]].astype(F32))
-    for c in outs:
-        c.wait()
+        settle(j ^ (2 + h), grads_of, ybr[h, :, piece(h, p, 0)[1]].astype(F32))
     for c in sends:
         c.wait_send()
     for k in range(NZ):
@@ -978,35 +965,28 @@
 
 def deliver_kernel(parts, *refs):
     n = len(parts)
-    srcs, dsts, bufs, ins, outs = refs[:n], refs[n:2 * n], refs[2 * n:3 * n], refs[3 * n], refs[3 * n + 1]
     moves, k = [], 0
-    for src, dst, buf, p in zip(srcs, dsts, bufs, parts):
+    for src, dst, p in zip(refs[:n], refs[n:2 * n], parts):
         step = src.shape[0] // p
         for i in range(p):
             at = pl.ds(i * step, step)
-            moves.append((pltpu.make_async_copy(src.at[at], buf.at[at], ins.at[k]),
-                          pltpu.make_async_copy(buf.at[at], dst.at[at], outs.at[k])))
+            moves.append(pltpu.make_async_copy(src.at[at], dst.at[at], refs[2 * n].at[k]))
             k += 1
-    for a, _ in moves:
+    for a in moves:
         a.start()
-    for a, b in moves:
+    for a in moves:
         a.wait()
-        b.start()
-    for _, b in moves:
-        b.wait()
 
 
 def deliver(*arrays):
-    parts = [8, 2, 2]
-    anyspec = pl.BlockSpec(memory_space=pl.ANY)
+    parts = [4, 1, 1]
     return pl.pallas_call(
         functools.partial(deliver_kernel, parts),
         out_shape=[jax.ShapeDtypeStruct(a.shape, a.dtype) for a in arrays],
-        in_specs=[anyspec] * len(arrays),
-        out_specs=[anyspec] * len(arrays),
-        scratch_shapes=[pltpu.VMEM(a.shape, a.dtype) for a in arrays]
-        + [pltpu.SemaphoreType.DMA((sum(parts),)), pltpu.SemaphoreType.DMA((sum(parts),))],
-        compiler_params=pltpu.CompilerParams(vmem_limit_bytes=67043328),
+        in_specs=[pl.BlockSpec(memory_space=pltpu.VMEM)] * len(arrays),
+        out_specs=[pl.BlockSpec(memory_space=pl.ANY)] * len(arrays),
+        scratch_shapes=[pltpu.SemaphoreType.DMA((sum(parts),))],
+        compiler_params=pltpu.CompilerParams(vmem_limit_bytes=1 << 20),
     )(*arrays)
 
 
@@ -1034,12 +1014,12 @@
     q_grad, kw, vw = pl.pallas_call(
         functools.partial(plane_kernel, cfg),
         out_shape=(
-            jax.ShapeDtypeStruct((T * R, QW), BF16),
-            jax.ShapeDtypeStruct((FB, kv_width), F32),
-            jax.ShapeDtypeStruct((FB, kv_width), F32),
+            V((T * R, QW), BF16),
+            V((FB, kv_width), F32),
+            V((FB, kv_width), F32),
         ),
         in_specs=[anyspec] * 7,
-        out_specs=(anyspec,) * 3,
+        out_specs=(vm,) * 3,
         scratch_shapes=[
             V((T * R, JW), BF16), V((T * R, JW), BF16),
             V((NR, HEAD_WIDTH), BF16), V((NR, HEAD_WIDTH), BF16),
@@ -1049,19 +1029,18 @@
             V((8, NR), F32), V((NZ, 8, NR), F32), V((8, NR), F32), V((8, NR), jnp.int32),
             V((NK, W2), BF16), V((2, NK, HEAD_WIDTH), BF16),
             V((HEAD_WIDTH, M * RZ), F32), V((T * R, JW), BF16),
-            V((NZ, RZ, JW), BF16), V((G, T * R, JW), BF16),
+            V((NZ, RZ, JW), BF16),
             V((G, 8, NR), F32), V((HEAD_WIDTH, NK), BF16),
-            V((2, FB, kv_width), F32), D((2, 4)),
             pltpu.SMEM(lengths.shape, jnp.int32), pltpu.SMEM(frame_range.shape[::-1], jnp.int32),
             V((2 * NZ, 2 * FB, W2), F32), V((2, NZ, 2 * FB, W2), BF16), V((2, NZ, 2, 2 * FB, W2), BF16),
             V((2, FB, W2), BF16), V((2, FB, W2), BF16),
             D((6,)), D((NZ, 2)),
         ] + pairs,
         compiler_params=pltpu.CompilerParams(
-            collective_id=0, has_side_effects=True, vmem_limit_bytes=67043328
+            collective_id=0, has_side_effects=True, vmem_limit_bytes=67043328 - T * R * QW * 2 - 8 * FB * kv_width - (1 << 18)
         ),
     )(text_queries, text_grads, vision_keys, video_value_rows, vision, lengths, frame_range.T)
-    return deliver(q_grad, kw, vw)
+    return deliver(*[pltpu.with_memory_space_constraint(a, pltpu.VMEM) for a in (q_grad, kw, vw)])
 
 
 def solution(mesh):

time: 95.7 us -> 93.9 us (0.981)
  Pallas kernels: 94.7 us -> 92.9 us
    pallas_call x1, Pallas kernels: 2.81 us -> 1.71 us  [deliver(): pl.pallas_call(functools.partial(deliver_kernel, parts), out_shape=[jax.S...]
where the time goes in v5:
time: 93.9 us; the launch traced here: 93.7 us
  Pallas kernels  92.9 us (99%)
    pallas_call x1, Pallas kernels, plane_shards(): pl.pallas_call(functools.partial(plane_kernel, cfg), out_shape=(V((T * R,...  91.2 us

profile of v5, /device:TPU:0, one launch (start us, length us, event | category | flops | bytes accessed | tf_op | source)
XLA Modules:
  0.0 93.7 jit_solution(16999277049618647935)
XLA Ops:
  0.6 91.2 %shard_map.94 = (bf16[256,4096]{1,0:T(8,128)(2,1)S(1)}, f32[256,512]{1,0:T(8,128)S(1)}, f32[256,512]{1,0:T(8,128)S(1)}) custom-call(bf16[16,4096]{1,0:T(8,128)(2,1)} %q_in.1, bf16[16,4096]{1,0:T(8,128)(2,1)} %g_in.1, bf16[512,512]{1,0:T(8,128)(2,1)} %k_in.1, bf16[512,512]{1,0:T(8,128)(2,1)} %v_in.1, bf16[512,4096]{1,0:T(8,128)(2,1)} %x_in.1, s32[8]{0:T(128)} %lens_in.1, ...), custom_call_target="tpu_custom_call" | custom-call | tf_op jit(solution)/shard_map/pallas_call | solution.py:1014
  91.8 1.7 %shard_map.95 = (bf16[256,4096]{1,0:T(8,128)(2,1)}, f32[256,512]{1,0:T(8,128)}, f32[256,512]{1,0:T(8,128)}) custom-call(bf16[256,4096]{1,0:T(8,128)(2,1)S(1)} %get-tuple-element.6.refs_0_, f32[256,512]{1,0:T(8,128)S(1)} %get-tuple-element.7.refs_1_, f32[256,512]{1,0:T(8,128)S(1)} %get-tuple-element.8.refs_2_), custom_call_target="tpu_custom_call" | custom-call | tf_op jit(solution)/shard_map/pallas_call | solution.py:983

commit v6 on v5

--- a/solution.py
+++ b/solution.py
@@ -912,6 +912,7 @@
     later(1, 0)
     gather(2)
     first(2, 0)
+    early = len(sends)
     shared_dq()
     first(2, 1, 1)
     later(0, 1, 1)
@@ -928,26 +929,33 @@
     y_pass(0, 1, 2)
     y_pass(1, 2, 1)
     later(2, 1, 1)
+    y_pass(2, 2, 1)
+    later(0, 1, 0)
+    y_pass(3, 2, 1)
     finish(0)
-    later(0, 1, 0)
-    y_pass(2, 2, 1)
-    y_pass(3, 2, 1)
     later(1, 1, 0)
     later(2, 1, 0)
+    for c in sends[:early]:
+        c.wait_send()
+    for k in range(NZ):
+        zq_each(lambda c: c.wait_send(), band(NZ - 1 - k), False)
+    for d in range(1, NZ):
+        d_copy(far(d)[0], z).wait_send()
+    for zb in range(NZ):
+        for d in range(1, NZ):
+            s_copy(zb, far(d)[0], z, far(d)[2]).wait_send()
+    finish(1, 1)
+    finish(1, 0)
     for u in range(1, 4):
         y_copy(u, near(1)[0], me, 0).wait_recv()
     y_copy(0, near(2)[0], me, 1).wait_recv()
-    finish(1, 1)
-    finish(1, 0)
     for u in range(4):
         y_copy(u, near(3)[0], me, 2).wait_recv()
     for h, p, grads_of in ((0, 0, (0, 1)), (1, 1, (1,)), (1, 0, (0,))):
         e_copy(h, p, me).wait_recv()
         settle(j ^ (2 + h), grads_of, ybr[h, :, piece(h, p, 0)[1]].astype(F32))
-    for c in sends:
+    for c in sends[early:]:
         c.wait_send()
-    for k in range(NZ):
-        zq_each(lambda c: c.wait_send(), band(NZ - 1 - k), False)
     for u in range(2):
         a_own(u, lambda c: c.wait_send())
         pl.when(inner)(lambda: a_onward(u, lambda c: c.wait_send()))
@@ -956,11 +964,6 @@
         for h, p in ((0, 0), (1, 0), (1, 1)):
             for i in range(2):
                 c_copy(side, b, h, p, i, peer).wait_send()
-    for d in range(1, NZ):
-        d_copy(far(d)[0], z).wait_send()
-    for zb in range(NZ):
-        for d in range(1, NZ):
-            s_copy(zb, far(d)[0], z, far(d)[2]).wait_send()
 
 
 def deliver_kernel(parts, *refs):
@@ -979,7 +982,7 @@
 
 
 def deliver(*arrays):
-    parts = [4, 1, 1]
+    parts = [8, 2, 2]
     return pl.pallas_call(
         functools.partial(deliver_kernel, parts),
         out_shape=[jax.ShapeDtypeStruct(a.shape, a.dtype) for a in arrays],

time: 93.9 us -> 93.4 us (level)
  no operation moved by 1% of the time
where the time goes in v6:
time: 93.4 us; the launch traced here: 93.3 us
  Pallas kernels  92.5 us (99%)
    pallas_call x1, Pallas kernels, plane_shards(): pl.pallas_call(functools.partial(plane_kernel, cfg), out_shape=(V((T * R,...  90.7 us

profile of v6, /device:TPU:0, one launch (start us, length us, event | category | flops | bytes accessed | tf_op | source)
XLA Modules:
  0.0 93.3 jit_solution(878162878357054939)
XLA Ops:
  0.6 90.7 %shard_map.94 = (bf16[256,4096]{1,0:T(8,128)(2,1)S(1)}, f32[256,512]{1,0:T(8,128)S(1)}, f32[256,512]{1,0:T(8,128)S(1)}) custom-call(bf16[16,4096]{1,0:T(8,128)(2,1)} %q_in.1, bf16[16,4096]{1,0:T(8,128)(2,1)} %g_in.1, bf16[512,512]{1,0:T(8,128)(2,1)} %k_in.1, bf16[512,512]{1,0:T(8,128)(2,1)} %v_in.1, bf16[512,4096]{1,0:T(8,128)(2,1)} %x_in.1, s32[8]{0:T(128)} %lens_in.1, ...), custom_call_target="tpu_custom_call" | custom-call | tf_op jit(solution)/shard_map/pallas_call | solution.py:1017
  91.3 1.8 %shard_map.95 = (bf16[256,4096]{1,0:T(8,128)(2,1)}, f32[256,512]{1,0:T(8,128)}, f32[256,512]{1,0:T(8,128)}) custom-call(bf16[256,4096]{1,0:T(8,128)(2,1)S(1)} %get-tuple-element.6.refs_0_, f32[256,512]{1,0:T(8,128)S(1)} %get-tuple-element.7.refs_1_, f32[256,512]{1,0:T(8,128)S(1)} %get-tuple-element.8.refs_2_), custom_call_target="tpu_custom_call" | custom-call | tf_op jit(solution)/shard_map/pallas_call | solution.py:986
